TPU v7x, 16 devices: a whole 2x2x2 slice. The times are simulated.
16 devices in a mesh: nodes: 16 (over z, y, x, core).
Axes of the slice: x: 2, y: 2, z: 2, core: 2. Of those that a mesh axis runs over, the one named last changes fastest.
Arguments:
- adjacency: bfloat16 [16384, 16384], P('nodes')
- features: bfloat16 [16384, 128], P('nodes')
- w_one: float32 [128, 256], replicated
- w_two: float32 [256, 349], replicated
- labels: int32 [16384], P('nodes')
- label_mask: int32 [16384], P('nodes')
Outputs:
- output 1: float32 [], replicated
- output 2: float32 [128, 256], replicated
- output 3: float32 [256, 349], replicated
All inputs are finite; a program needn't handle non-finite values.
Results may differ from a plain program's by a relative error of at most 0.00164724.
Values are sent between devices in bfloat16 or wider.
A program may use at most 1 GiB of HBM per device.

v0:
```python
import jax
import jax.numpy as jnp
from jax import lax
from jax.sharding import PartitionSpec as P


def contract_rows(left, right):
    return lax.dot_general(left, right, (((0,), (0,)), ((), ())), preferred_element_type=jnp.float32)


def solution(mesh):
    node_axis = mesh.axis_names[0]

    def local_step(adj_rows, feat_rows, w_one, w_two, label_rows, mask_rows):
        classes = w_two.shape[1]
        w_one_b = w_one.astype(jnp.bfloat16)
        w_two_b = w_two.astype(jnp.bfloat16)
        y_one = jnp.dot(feat_rows, w_one_b, preferred_element_type=jnp.float32).astype(jnp.bfloat16)
        y_one_all = lax.all_gather(y_one, node_axis, tiled=True)
        z_one = jnp.dot(adj_rows, y_one_all, preferred_element_type=jnp.float32)
        h_one = jnp.maximum(z_one, 0.0).astype(jnp.bfloat16)
        y_two = jnp.dot(h_one, w_two_b, preferred_element_type=jnp.float32).astype(jnp.bfloat16)
        y_two_all = lax.all_gather(y_two, node_axis, tiled=True)
        z_two = jnp.dot(adj_rows, y_two_all, preferred_element_type=jnp.float32)
        mask_f = mask_rows.astype(jnp.float32)
        label_count = lax.psum(jnp.sum(mask_f), node_axis)
        log_norm = jax.nn.logsumexp(z_two, axis=1)
        onehot = (label_rows[:, None] == jnp.arange(classes, dtype=jnp.int32)[None, :]).astype(jnp.float32)
        picked = jnp.sum(z_two * onehot, axis=1)
        loss_value = lax.psum(jnp.sum(mask_f * (log_norm - picked)), node_axis) / label_count
        soft_probs = jnp.exp(z_two - log_norm[:, None])
        g_two = ((soft_probs - onehot) * (mask_f / label_count)[:, None]).astype(jnp.bfloat16)
        part_y2 = contract_rows(adj_rows, g_two)
        grad_y2 = lax.psum_scatter(part_y2, node_axis, scatter_dimension=0, tiled=True).astype(jnp.bfloat16)
        grad_two = lax.psum(contract_rows(h_one, grad_y2), node_axis)
        grad_h1 = lax.dot_general(grad_y2, w_two_b, (((1,), (1,)), ((), ())), preferred_element_type=jnp.float32)
        grad_z1 = jnp.where(z_one > 0.0, grad_h1, 0.0).astype(jnp.bfloat16)
        part_y1 = contract_rows(adj_rows, grad_z1)
        grad_y1 = lax.psum_scatter(part_y1, node_axis, scatter_dimension=0, tiled=True).astype(jnp.bfloat16)
        grad_one = lax.psum(contract_rows(feat_rows, grad_y1), node_axis)
        return loss_value, grad_one, grad_two

    return jax.shard_map(local_step, mesh=mesh, in_specs=(P(node_axis, None), P(node_axis, None), P(None, None), P(None, None), P(node_axis), P(node_axis)), out_specs=(P(), P(None, None), P(None, None)), check_vma=False)
```

profile of v0, /device:TPU:0, one launch (start us, length us, event | category | flops | bytes accessed | tf_op | source)
XLA Modules:
  0.0 739.6 jit_solution(13884297141582099835)
XLA Ops:
  7.2 0.9 copy-done
  8.1 2.0 convolution_convert_fusion.1
  10.2 51.6 %all-gather.3.cloned.1.call-done = bf16[16384,256]{1,0:T(8,128)(2,1)} async-done(((bf16[1024,256]{1,0:T(8,128)(2,1)}), bf16[16384,256]{1,0:T(8,128)(2,1)}) %all-gather.3.cloned.1.call-update) | async-done | bytes 8388624 | tf_op jit(solution)/shard_map/all_gather | solution.py:19
  61.8 16.6 %fusion.29 = f32[256,1024]{1,0:T(8,128)S(1)} fusion(bf16[16384,256]{1,0:T(8,128)(2,1)} %all-gather.3.cloned.1.call-done, bf16[1024,16384]{1,0:T(8,128)(2,1)} %param.6), kind=kOutput, calls=%fused_computation.42 | convolution fusion | flops 8589934592 | bytes 42991616 | tf_op jit(solution)/shard_map/dot_general | solution.py:20
  78.4 1.4 convolution_convert_fusion
  79.9 62.4 %all-gather.5.cloned.1.call-done = bf16[16384,349]{1,0:T(8,128)(2,1)} async-done(((bf16[1024,349]{1,0:T(8,128)(2,1)}), bf16[16384,349]{1,0:T(8,128)(2,1)}) %all-gather.5.cloned.1.call-update) | async-done | bytes 11436048 | tf_op jit(solution)/shard_map/all_gather | solution.py:23
  142.3 21.0 %fusion.28 = (f32[1024]{0:T(1024)S(1)}, f32[349,1024]{1,0:T(8,128)S(1)}) fusion(bf16[16384,349]{1,0:T(8,128)(2,1)} %all-gather.5.cloned.1.call-done, bf16[1024,16384]{1,0:T(8,128)(2,1)} %param.6), kind=kOutput, calls=%fused_computation.41 | convolution fusion | flops 11710853120 | bytes 46424064 | tf_op jit(solution)/shard_map/dot_general | solution.py:24
  163.4 0.4 fusion.2
  163.8 0.3 copy-done.3
  164.0 0.6 convert_reduce_fusion
  164.6 31.9 %all-reduce = (f32[]{:T(128)}, f32[]{:T(128)}) all-reduce(f32[]{:T(128)} %get-tuple-element.9, f32[]{:T(128)} %get-tuple-element.8), channel_id=1, replica_groups=mesh['nodes'=16] {'nodes'}, use_global_device_ids=true, to_apply=%region_4.0 | all-reduce | flops 2 | bytes 16 | tf_op jit(solution)/shard_map/psum | solution.py:30
  196.6 0.6 convert_divide_fusion
  197.3 25.7 %convolution_bitcast_fusion = f32[16384,349]{0,1:T(8,128)} fusion(bf16[1024,16384]{1,0:T(8,128)(2,1)} %param.6, f32[349,1024]{1,0:T(8,128)S(1)} %get-tuple-element.16, f32[1024]{0:T(1024)S(1)} %convert_divide_fusion, f32[1024]{0:T(1024)S(1)} %get-tuple-element.14, s32[1024]{0:T(1024)S(1)} %copy-done.4), kind=kOutput, calls=%fused_computation | convolution fusion | flops 11712641024 | bytes 57868288 | tf_op jit(solution)/shard_map/dot_general | solution.py:8
  223.0 0.2 reduce-scatter.5.cloned.1.call-start
  223.2 241.4 %reduce-scatter.3.cloned.1.call-done = f32[1024,349]{0,1:T(8,128)} async-done(((f32[16384,349]{0,1:T(8,128)}), f32[1024,349]{0,1:T(8,128)}) %reduce-scatter.3.cloned.1.call-update) | async-done | bytes 1429520 | tf_op jit(solution)/shard_map/reduce_scatter | solution.py:34
  464.7 19.1 %convolution_bitcast_fusion.1 = f32[16384,256]{0,1:T(8,128)} fusion(bf16[1024,16384]{1,0:T(8,128)(2,1)} %param.6, f32[256,1024]{1,0:T(8,128)S(1)} %fusion.29, f32[1024,349]{0,1:T(8,128)} %reduce-scatter.3.cloned.1.call-done, f32[256,349]{0,1:T(8,128)S(1)} %copy-done.1), kind=kOutput, calls=%fused_computation.1 | convolution fusion | flops 8774144000 | bytes 53167104 | tf_op jit(solution)/shard_map/dot_general | solution.py:8
  483.8 0.0 all-reduce.4.cloned.1.call-start
  483.8 1.3 copy-done.2
  485.1 1.1 fusion.17
  486.2 173.2 %reduce-scatter.5.cloned.1.call-done = f32[1024,256]{0,1:T(8,128)} async-done(((f32[16384,256]{0,1:T(8,128)}), f32[1024,256]{0,1:T(8,128)}) %reduce-scatter.5.cloned.1.call-update) | async-done | bytes 1048592 | tf_op jit(solution)/shard_map/reduce_scatter | solution.py:39
  659.4 2.2 convolution_bitcast_fusion.2
  662.9 65.7 %all-reduce.4.cloned.1.call-done = (f32[128,256]{0,1:T(8,128)}, f32[256,349]{0,1:T(8,128)}) async-done(((f32[128,256]{0,1:T(8,128)}, f32[256,349]{0,1:T(8,128)}), (f32[128,256]{0,1:T(8,128)}, f32[256,349]{0,1:T(8,128)})) %all-reduce.4.cloned.1.call-update) | async-done | bytes 488464 | tf_op jit(solution)/shard_map/psum | solution.py:40
  728.6 1.7 copy.9
  730.2 1.7 copy.12
  (16 shorter events, 0.2 us)
Async XLA Ops:
  7.2 1.0 copy-start
  7.2 54.6 %all-gather.3.cloned.1.call-start = ((), (), s32[]{:S(2)}) async-start(), calls=%async_computation.2 | async-start | bytes 8912896 | tf_op jit(solution)/shard_map/all_gather | solution.py:19
  10.2 68.3 %copy-start.1 = (f32[256,349]{0,1:T(8,128)S(1)}, f32[256,349]{0,1:T(8,128)}, u32[]{:S(2)}) copy-start(f32[256,349]{0,1:T(8,128)} %param.9) | copy-start | bytes 1072132
  10.2 132.1 %all-gather.5.cloned.1.call-start = ((), (), s32[]{:S(2)}) async-start(), calls=%async_computation.3 | async-start | bytes 13369344 | tf_op jit(solution)/shard_map/all_gather | solution.py:23
  79.9 83.5 %copy-start.4 = (s32[1024]{0:T(1024)S(1)}, s32[1024]{0:T(1024)}, u32[]{:S(2)}) copy-start(s32[1024]{0:T(1024)} %param.10) | copy-start | bytes 12292
  79.9 384.8 %reduce-scatter.3.cloned.1.call-start = ((), (), s32[]{:S(2)}) async-start(), calls=%async_computation.4 | async-start | bytes 24510464 | tf_op jit(solution)/shard_map/reduce_scatter | solution.py:34
  163.3 0.7 copy-start.3
  223.0 436.4 %reduce-scatter.5.cloned.1.call-start = ((), (), s32[]{:S(2)}) async-start(), calls=%async_computation.5 | async-start | bytes 17825792 | tf_op jit(solution)/shard_map/reduce_scatter | solution.py:39
  483.7 1.4 copy-start.2
  483.8 244.8 %all-reduce.4.cloned.1.call-start = ((), (), s32[]{:S(2)}) async-start(), calls=%async_computation.6 | async-start | bytes 983040 | tf_op jit(solution)/shard_map/psum | solution.py:40
Sparse Core Ops, SparseCore 0:
  10.3 51.4 all-gather.2
  80.0 62.2 all-gather.4
  223.1 241.5 reduce-scatter.2
  483.9 175.4 reduce-scatter.4
  664.2 64.2 all-reduce.3
where the time goes:
time: 740 us
  waiting for transfers between devices  594 us (80%)
  matrix products  89.1 us (12%)
  blocking collectives  31.9 us (4%)
  between operations  16.3 us (2%)
    reduce_scatter x1, waiting for transfers between devices, local_step(): lax.psum_scatter(part_y2, node_axis, scatter_dimension=0, tiled=True)  241 us
    reduce_scatter x1, waiting for transfers between devices, local_step(): lax.psum_scatter(part_y1, node_axis, scatter_dimension=0, tiled=True)  173 us
    psum x1, waiting for transfers between devices, local_step(): grad_one = lax.psum(contract_rows(feat_rows, grad_y1), node_axis)  65.7 us
    all_gather x1, waiting for transfers between devices, local_step(): y_two_all = lax.all_gather(y_two, node_axis, tiled=True)  62.4 us
    all_gather x1, waiting for transfers between devices, local_step(): y_one_all = lax.all_gather(y_one, node_axis, tiled=True)  51.6 us
    dot_general x4, matrix products, contract_rows(): lax.dot_general(left, right, (((0,), (0,)), ((), ())), preferred_element_...  48.1 us
    psum x1, blocking collectives, local_step(): lax.psum(jnp.sum(mask_f * (log_norm - picked)), node_axis) / label_count  31.9 us
    dot_general x1, matrix products, local_step(): z_two = jnp.dot(adj_rows, y_two_all, preferred_element_type=jnp.float32)  21 us
  transfers between devices with their start and end apart: 5, of which 5 were waited for; matrix products, arithmetic and copies ran while one was open for 0% of the time, Pallas kernels for 0%

commit v1 on v0

v1 whole, which is shorter than its diff:
```python
import functools

import jax
import jax.numpy as jnp
from jax import lax
from jax.experimental import pallas as pl
from jax.experimental.pallas import tpu as pltpu
from jax.sharding import PartitionSpec as P

F32 = jnp.float32
BF16 = jnp.bfloat16
MESH = pl.DeviceIdType.MESH
DEVICES = 16
UNITS = 4
LANES = 128
CHUNK = 512


def dot(a, b):
    return jnp.dot(a, b, preferred_element_type=F32)


def dot_tn(a, b):
    return lax.dot_general(a, b, (((0,), (0,)), ((), ())), preferred_element_type=F32)


def dot_nt(a, b):
    return lax.dot_general(a, b, (((1,), (1,)), ((), ())), preferred_element_type=F32)


def loop(n, fn):
    lax.fori_loop(0, n, lambda i, c: (fn(i), c)[1], 0)


def step_kernel(classes, adj, x_ref, w1_ref, w2_ref, lab_ref, msk_ref,
                loss_out, g1_out, g2_out,
                a_v, gb, hb, acc1, acc2, ys1, ys2, hown, e2own, w1b, w2b,
                w2acc, w2rcv, w2f, w1p, w1r, w1f, cnt_src, cnt_rcv, loss_acc,
                a_sem, rsem, ssem, sib_rsem, sib_ssem, cs_sem, cr_sem,
                w2s_sem, w2r_sem, w1s_sem, w1r_sem, w1gs_sem, w1gr_sem):
    rows = x_ref.shape[0]
    fin = x_ref.shape[1]
    unit = rows // UNITS
    hid = w1_ref.shape[1]
    cpad = w2b.shape[0]
    me = lax.axis_index("nodes")
    core = me % 2
    sib = me + 1 - 2 * core
    bit = [(me // v) % 2 for v in (2, 4, 8)]
    step = [v * (1 - 2 * b) for v, b in zip((2, 4, 8), bit)]
    own_d = [(1 - core) * step[r] + core * step[(r + 1) % 3] for r in range(3)]
    sib_d = [core * step[r] + (1 - core) * step[(r + 1) % 3] for r in range(3)]
    role_bit = [(1 - core) * bit[r] + core * bit[(r + 1) % 3] for r in range(3)]
    nbr = [me + d for d in own_d]

    def src_dev(base, deltas, hop, r):
        return base + deltas[r] + hop * deltas[(r + 2) % 3]

    anti = me + own_d[0] + own_d[1] + own_d[2]
    anti_sib = anti + 1 - 2 * core

    def remote(src, dst, ss, rs, dev):
        return pltpu.make_async_remote_copy(src_ref=src, dst_ref=dst, send_sem=ss, recv_sem=rs,
                                            device_id=(dev,), device_id_type=MESH)

    order = [me, sib]
    for hop in (0, 1):
        order += [src_dev(me, own_d, hop, r) for r in range(3)]
        order += [src_dev(sib, sib_d, hop, r) for r in range(3)]
    order += [anti, anti_sib]

    def a_cols(dev):
        return pl.ds(pl.multiple_of(dev * rows, rows), rows)

    def a_copy(i):
        return pltpu.make_async_copy(adj.at[:, a_cols(order[i])], a_v.at[:, a_cols(order[i])], a_sem.at[i])

    for i in range(DEVICES):
        a_copy(i).start()

    def rows_of(dev, q):
        return pl.ds(pl.multiple_of(dev * rows + q * unit, unit), unit)

    def uid(dev, q):
        return dev * UNITS + q

    for q in range(UNITS):
        gb[uid(me, q), :unit, :fin] = x_ref[q * unit:(q + 1) * unit, :]

    barrier = pltpu.get_barrier_semaphore()
    for i in range(1, DEVICES):
        pl.semaphore_signal(barrier, inc=1, device_id=((me + i) % DEVICES,), device_id_type=MESH)
    pl.semaphore_wait(barrier, DEVICES - 1)

    def pick(f, vals):
        return jnp.where(f == 0, vals[0], jnp.where(f == 1, vals[1], vals[2]))

    class Gather:
        def __init__(self, view, par):
            self.view, self.par = view, par

        def hop_copy(self, dev, q, to, sslot, rslot):
            v = self.view(dev, q)
            return remote(v, v, ssem.at[self.par, sslot], rsem.at[self.par, rslot], to)

        def sib_copy(self, dev, q, slot):
            v = self.view(dev, q)
            return remote(v, v, sib_ssem.at[self.par, slot], sib_rsem.at[self.par, slot], sib)

        def own_copies(self, q):
            return [self.hop_copy(me, q, nbr[r], r * 4 + q, r * 4 + q) for r in range(3)] + [self.sib_copy(me, q, 28 + q)]

        def start_own(self, q):
            for c in self.own_copies(q):
                c.start()

        def forward(self, q):
            return [self.hop_copy(src_dev(me, own_d, 0, r), q, nbr[(r + 1) % 3], 12 + r * 4 + q,
                                  12 + ((r + 1) % 3) * 4 + q) for r in range(3)]

        def last_forward(self, q):
            to = q % 3
            dev = pick((to + 2) % 3, [src_dev(me, own_d, 1, r) for r in range(3)])
            return self.hop_copy(dev, q, pick(to, nbr), 24 + q, 24 + q)

        def arrive(self, hop, q):
            for r in range(3):
                d = src_dev(me, own_d, hop, r)
                self.hop_copy(d, q, nbr[r], r * 4 + q, hop * 12 + r * 4 + q).wait_recv()

            @pl.when(hop == 0)
            def _():
                for c in self.forward(q):
                    c.start()

            @pl.when(hop == 1)
            def _():
                self.last_forward(q).start()
            for r in range(3):
                self.sib_copy(src_dev(me, own_d, hop, r), q, hop * 12 + r * 4 + q).start()

        def arrive_last(self, q):
            self.hop_copy(anti, q, nbr[0], 24 + q, 24 + q).wait_recv()
            self.sib_copy(anti, q, 24 + q).start()

        def sib_wait(self, hop, q):
            for r in range(3):
                self.sib_copy(src_dev(sib, sib_d, hop, r), q, hop * 12 + r * 4 + q).wait_recv()

        def sib_wait_own(self, q):
            self.sib_copy(sib, q, 28 + q).wait_recv()

        def sib_wait_last(self, q):
            self.sib_copy(anti_sib, q, 24 + q).wait_recv()

        def wait_sends(self):
            def body(q):
                for c in self.own_copies(q) + self.forward(q) + [self.last_forward(q)]:
                    c.wait_send()
                for slot in (q, 4 + q, 8 + q, 12 + q, 16 + q, 20 + q, 24 + q):
                    self.sib_copy(me, q, slot).wait_send()
            loop(UNITS, body)

    def phase(g, add, zero, finish, hook, first):
        def a_wait(lo, hi):
            if first:
                for i in range(lo, hi):
                    a_copy(i).wait()

        zero()

        def near(t):
            if first:
                @pl.when(t == 0)
                def _():
                    a_wait(0, 1)

            @pl.when(t == 1)
            def _():
                for q in range(UNITS):
                    g.sib_wait_own(q)
                a_wait(1, 2)
            dev = me + t * (sib - me)
            add([(dev, q) for q in range(UNITS)])
        loop(2, near)
        hook(-1, None)

        def group(i):
            hop, q, far = (i // 4) % 2, i % 4, i // 8

            @pl.when(far == 0)
            def _():
                g.arrive(hop, q)

            @pl.when(far == 1)
            def _():
                for j in range(3):
                    g.arrive_last(j)
            hook(None, i)

            def half(t):
                @pl.when(t == 1)
                def _():
                    @pl.when(far == 0)
                    def _():
                        g.sib_wait(hop, q)

                    @pl.when(far == 1)
                    def _():
                        for j in range(3):
                            g.sib_wait_last(j)
                if first:
                    for k, (lo, hi) in {(0, 0): (2, 5), (0, 1): (5, 8), (4, 0): (8, 11), (4, 1): (11, 14),
                                        (8, 0): (14, 15), (8, 1): (15, 16)}.items():
                        @pl.when((i == k[0]) & (t == k[1]))
                        def _(lo=lo, hi=hi):
                            a_wait(lo, hi)
                pairs = []
                for r in range(3):
                    o, s = src_dev(me, own_d, hop, r), src_dev(sib, sib_d, hop, r)
                    near_dev = o + t * (s - o)
                    far_dev = anti + t * (anti_sib - anti)
                    pairs.append((near_dev + far * (far_dev - near_dev), q + far * (r - q)))
                add(pairs)
            loop(2, half)
        loop(9, group)
        g.arrive_last(3)
        g.sib_wait_last(3)

        def last(m):
            @pl.when(m == UNITS - 1)
            def _():
                g.wait_sends()
            finish(m, [(anti, 3), (anti_sib, 3)])
        loop(UNITS, last)

    gx = Gather(lambda dev, q: gb.at[uid(dev, q), pl.ds(0, unit), pl.ds(0, fin)], 0)
    gh = Gather(lambda dev, q: hb.at[rows_of(dev, q)], 1)
    gg = Gather(lambda dev, q: gb.at[uid(dev, q)], 0)

    def mrows(m):
        return pl.ds(pl.multiple_of(m * unit, unit), unit)

    def chunk(c):
        return pl.ds(pl.multiple_of(c * CHUNK, CHUNK), CHUNK)

    for q in range(UNITS):
        gx.start_own(q)
    w1b[...] = w1_ref[...].astype(BF16)
    w2acc[...] = jnp.zeros_like(w2acc)
    w2acc[:classes, :] = w2_ref[...]
    w2b[...] = w2acc[:cpad, :].astype(BF16)

    partners = [sib] + nbr

    def cnt_copy(i):
        return remote(cnt_src.at[i], cnt_rcv.at[i], cs_sem.at[i], cr_sem.at[i], partners[i])

    local = jnp.sum(msk_ref[...].astype(F32), axis=1, keepdims=True)
    local = jnp.sum(local, axis=0, keepdims=True)
    cnt_src[0] = jnp.broadcast_to(local, (8, LANES))

    def hook1(pre, i):
        if i is None:
            cnt_copy(0).start()
            return
        for k in range(4):
            @pl.when(i == k + 1)
            def _(k=k):
                cnt_copy(k).wait_recv()
                cnt_src[k + 1] = cnt_src[k] + cnt_rcv[k]
                if k < 3:
                    cnt_copy(k + 1).start()

        @pl.when(i == 7)
        def _():
            for k in range(4):
                cnt_copy(k).wait_send()

    def zero1():
        acc1[...] = jnp.zeros_like(acc1)

    def y1(dev, q):
        return dot(gb[uid(dev, q), :unit, :fin], w1b[...]).astype(BF16)

    def add_rows(acc, pairs, operand):
        def body(c):
            s = chunk(c)
            v = acc[s, :]
            for j, (dev, q) in enumerate(pairs):
                v = v + dot(a_v[s, rows_of(dev, q)], operand(j))
            acc[s, :] = v
        loop(rows // CHUNK, body)

    def add1(pairs):
        for j, (dev, q) in enumerate(pairs):
            ys1[j] = y1(dev, q)
        add_rows(acc1, pairs, lambda j: ys1[j])

    def finish1(m, pairs):
        s = mrows(m)

        @pl.when(m == 0)
        def _():
            for j, (dev, q) in enumerate(pairs):
                ys1[j] = y1(dev, q)
        z = acc1[s, :]
        for j, (dev, q) in enumerate(pairs):
            z = z + dot(a_v[s, rows_of(dev, q)], ys1[j])
        acc1[s, :] = z
        h = jnp.maximum(z, 0.0).astype(BF16)
        hb[rows_of(me, m), :] = h
        hown[s, :] = h
        gh.start_own(m)

    phase(gx, add1, zero1, finish1, hook1, True)

    def zero2():
        acc2[...] = jnp.zeros_like(acc2)

    def y2(dev, q):
        return dot_nt(w2b[...], hb[rows_of(dev, q), :]).astype(BF16)

    def add_cols(acc, pairs, operand):
        def body(c):
            s = chunk(c)
            v = acc[:, s]
            for j, (dev, q) in enumerate(pairs):
                v = v + dot_nt(operand(j), a_v[s, rows_of(dev, q)])
            acc[:, s] = v
        loop(rows // CHUNK, body)

    def add2(pairs):
        for j, (dev, q) in enumerate(pairs):
            ys2[j] = y2(dev, q)
        add_cols(acc2, pairs, lambda j: ys2[j])

    loss_acc[...] = jnp.zeros_like(loss_acc)
    count = cnt_src[4][0:1, :]

    def finish2(m, pairs):
        s = mrows(m)

        @pl.when(m == 0)
        def _():
            for j, (dev, q) in enumerate(pairs):
                ys2[j] = y2(dev, q)
        z = acc2[:, s]
        for j, (dev, q) in enumerate(pairs):
            z = z + dot_nt(ys2[j], a_v[s, rows_of(dev, q)])
        acc2[:, s] = z
        for h in range(unit // LANES):
            at = pl.ds(pl.multiple_of(m * unit + h * LANES, LANES), LANES)
            zc = acc2[:, at]
            row = lax.broadcasted_iota(jnp.int32, (cpad, LANES), 0)
            zm = jnp.where(row < classes, zc, -jnp.inf)
            top = jnp.max(zm, axis=0, keepdims=True)
            log_norm = top + jnp.log(jnp.sum(jnp.exp(zm - top), axis=0, keepdims=True))
            which = m * (unit // LANES) + h
            hot = row == lab_ref[pl.ds(which, 1), :]
            mask = msk_ref[pl.ds(which, 1), :].astype(F32)
            picked = jnp.sum(jnp.where(hot, zc, 0.0), axis=0, keepdims=True)
            loss_acc[...] = loss_acc[...] + mask * (log_norm - picked)
            gr = (jnp.exp(zm - log_norm) - jnp.where(hot, 1.0, 0.0)) * (mask / count)
            gb[uid(me, m), :, h * LANES:(h + 1) * LANES] = gr.astype(BF16)
        gg.start_own(m)

    phase(gh, add2, zero2, finish2, lambda pre, i: None, False)

    def finish3(m, pairs):
        s = mrows(m)
        z = acc2[:, s]
        for dev, q in pairs:
            z = z + dot_nt(gb[uid(dev, q)], a_v[s, rows_of(dev, q)])
        e = z.astype(BF16)
        e2own[:, s] = e
        gz = dot_tn(e, w2b[...])
        hb[rows_of(me, m), :] = jnp.where(acc1[s, :] > 0.0, gz, 0.0).astype(BF16)
        gh.start_own(m)

    phase(gg, lambda pairs: add_cols(acc2, pairs, lambda j: gb[uid(*pairs[j])]), zero2, finish3,
          lambda pre, i: None, False)

    total_rows = w2acc.shape[0]
    size = [total_rows // 2, total_rows // 4, total_rows // 8, total_rows // 16]
    bits = [core] + role_bit
    base = [0]
    for i in range(4):
        base.append(base[i] + bits[i] * size[i])
    roff = [0, size[0], size[0] + size[1], size[0] + size[1] + size[2]]

    def w2rows(start, n):
        return pl.ds(pl.multiple_of(start, 8), n)

    def w2_scatter(i):
        out = w2acc.at[w2rows(base[i] + (1 - bits[i]) * size[i], size[i])]
        return remote(out, w2rcv.at[pl.ds(roff[i], size[i])], w2s_sem.at[i], w2r_sem.at[i], partners[i])

    def w2_gather(i):
        out = w2f.at[w2rows(base[i + 1], size[i])]
        return remote(out, out, w2s_sem.at[4 + i], w2r_sem.at[4 + i], partners[i])

    def w2_gather_in(i):
        out = w2f.at[w2rows(base[i] + (1 - bits[i]) * size[i], size[i])]
        return remote(out, out, w2s_sem.at[4 + i], w2r_sem.at[4 + i], partners[i])

    def hook4(pre, i):
        if i is None:
            w2acc[...] = jnp.zeros_like(w2acc)
            w2acc[:cpad, :] = dot(e2own[...], hown[...])
            w2acc[total_rows - 1:, :LANES] = loss_acc[...]
            return

        @pl.when(i == 0)
        def _():
            w2_scatter(0).start()
        for k in range(4):
            @pl.when(i == k + 1)
            def _(k=k):
                w2_scatter(k).wait_recv()
                mine = w2rows(base[k + 1], size[k])
                into = w2acc if k < 3 else w2f
                into[mine, :] = w2acc[mine, :] + w2rcv[roff[k]:roff[k] + size[k], :]
                w2_scatter(k).wait_send()
                (w2_scatter(k + 1) if k < 3 else w2_gather(3)).start()
        for k in range(3):
            @pl.when(i == k + 5)
            def _(j=3 - k):
                w2_gather_in(j).wait_recv()
                w2_gather(j).wait_send()
                w2_gather(j - 1).start()

    def finish4(m, pairs):
        s = mrows(m)
        z = acc1[s, :]
        for dev, q in pairs:
            z = z + dot(a_v[s, rows_of(dev, q)], hb[rows_of(dev, q), :])
        part = dot_tn(x_ref[s, :], z.astype(BF16))
        w1p[...] = w1p[...] + part

    w1p[...] = jnp.zeros_like(w1p)
    phase(gh, lambda pairs: add_rows(acc1, pairs, lambda j: hb[rows_of(*pairs[j]), :]), zero1, finish4, hook4, False)

    sl = fin // DEVICES

    def w1rows(dev):
        return pl.ds(pl.multiple_of(dev * sl, sl), sl)

    def w1_scatter(i):
        dev = (me + i) % DEVICES
        return remote(w1p.at[w1rows(dev)], w1r.at[i], w1s_sem.at[i], w1r_sem.at[i], dev)

    def w1_gather(i):
        dev = (me + i) % DEVICES
        return remote(w1f.at[w1rows(me)], w1f.at[w1rows(me)], w1gs_sem.at[i], w1gr_sem.at[i], dev)

    def w1_gather_in(i):
        dev = (me + DEVICES - i) % DEVICES
        return remote(w1f.at[w1rows(dev)], w1f.at[w1rows(dev)], w1gs_sem.at[i], w1gr_sem.at[i], dev)

    for i in range(1, DEVICES):
        w1_scatter(i).start()
    w2_gather_in(0).wait_recv()
    w2_gather(0).wait_send()
    g2_out[...] = w2f[:classes, :]
    loss_out[0, 0] = jnp.sum(w2f[total_rows - 1:, :LANES] / cnt_src[4][0:1, :])
    total = w1p[w1rows(me), :]
    for i in range(1, DEVICES):
        w1_scatter(i).wait_recv()
    for i in range(1, DEVICES):
        total = total + w1r[i]
    w1f[w1rows(me), :] = total
    for i in range(1, DEVICES):
        w1_scatter(i).wait_send()
    for i in range(1, DEVICES):
        w1_gather(i).start()
    for i in range(1, DEVICES):
        w1_gather_in(i).wait_recv()
    g1_out[...] = w1f[...]
    for i in range(1, DEVICES):
        w1_gather(i).wait_send()


def solution(mesh):
    axis = mesh.axis_names[0]

    def local_step(adj, x, w1, w2, labels, mask):
        rows, nodes = adj.shape
        fin, hid = w1.shape
        classes = w2.shape[1]
        unit = rows // UNITS
        cpad = -(-classes // 16) * 16
        total_rows = -(-(cpad + 1) // LANES) * LANES
        dma = pltpu.SemaphoreType.DMA
        vm = pl.BlockSpec(memory_space=pltpu.VMEM)
        loss, g1, g2 = pl.pallas_call(
            functools.partial(step_kernel, classes),
            out_shape=(jax.ShapeDtypeStruct((1, 1), F32),
                       jax.ShapeDtypeStruct((fin, hid), F32),
                       jax.ShapeDtypeStruct((classes, hid), F32)),
            in_specs=[pl.BlockSpec(memory_space=pl.ANY)] + [vm] * 5,
            out_specs=(pl.BlockSpec(memory_space=pltpu.SMEM), vm, vm),
            scratch_shapes=[
                pltpu.VMEM((rows, nodes), BF16),
                pltpu.VMEM((nodes // unit, cpad, unit), BF16),
                pltpu.VMEM((nodes, hid), BF16),
                pltpu.VMEM((rows, hid), F32),
                pltpu.VMEM((cpad, rows), F32),
                pltpu.VMEM((UNITS, unit, hid), BF16),
                pltpu.VMEM((UNITS, cpad, unit), BF16),
                pltpu.VMEM((rows, hid), BF16),
                pltpu.VMEM((cpad, rows), BF16),
                pltpu.VMEM((fin, hid), BF16),
                pltpu.VMEM((cpad, hid), BF16),
                pltpu.VMEM((total_rows, hid), F32),
                pltpu.VMEM((total_rows, hid), F32),
                pltpu.VMEM((total_rows, hid), F32),
                pltpu.VMEM((fin, hid), F32),
                pltpu.VMEM((DEVICES, fin // DEVICES, hid), F32),
                pltpu.VMEM((fin, hid), F32),
                pltpu.VMEM((5, 8, LANES), F32),
                pltpu.VMEM((4, 8, LANES), F32),
                pltpu.VMEM((1, LANES), F32),
                dma((DEVICES,)),
                dma((2, 28)), dma((2, 28)), dma((2, 32)), dma((2, 32)),
                dma((4,)), dma((4,)), dma((8,)), dma((8,)),
                dma((DEVICES,)), dma((DEVICES,)), dma((DEVICES,)), dma((DEVICES,)),
            ],
            compiler_params=pltpu.CompilerParams(collective_id=0, has_side_effects=True,
                                                 vmem_limit_bytes=67043328),
            name="gcn_step",
        )(adj, x, w1, w2.T, labels.reshape(rows // LANES, LANES), mask.reshape(rows // LANES, LANES))
        return loss[0, 0], g1, g2.T

    return jax.shard_map(local_step, mesh=mesh,
                         in_specs=(P(axis, None), P(axis, None), P(None, None), P(None, None), P(axis), P(axis)),
                         out_specs=(P(), P(None, None), P(None, None)), check_vma=False)
```

time: 740 us -> 171 us (0.23)
  waiting for transfers between devices: 594 us -> 0 us
  Pallas kernels: 0 us -> 165 us
  matrix products: 89.1 us -> 0 us
  blocking collectives: 31.9 us -> 0 us
  between operations: 16.3 us -> 2.38 us
    reduce_scatter x2 -> x0, waiting for transfers between devices: 415 us -> none  [the longest x1 241 us: local_step(): lax.psum_scatter(part_y2, node_axis, scatter_dimension=0, tiled=True)]
    pallas_call x0 -> x1, Pallas kernels: none -> 165 us  [local_step(): pl.pallas_call(functools.partial(step_kernel, classes), out_shape=(jax.Sh...]
    all_gather x2 -> x0, waiting for transfers between devices: 114 us -> none  [the longest x1 62.4 us: local_step(): y_two_all = lax.all_gather(y_two, node_axis, tiled=True)]
    dot_general x8 -> x0, matrix products: 89.1 us -> none  [the longest x4 48.1 us: contract_rows(): lax.dot_general(left, right, (((0,), (0,)), ((), ())), preferred_element_...]
    psum x1 -> x0, waiting for transfers between devices: 65.7 us -> none  [local_step(): grad_one = lax.psum(contract_rows(feat_rows, grad_y1), node_axis)]
    psum x1 -> x0, blocking collectives: 31.9 us -> none  [local_step(): lax.psum(jnp.sum(mask_f * (log_norm - picked)), node_axis) / label_count]
  transfers between devices with their start and end apart: 5 -> 0, of which waited for: 5 -> 0; matrix products, arithmetic and copies ran while one was open for 0% -> 0% of each run, Pallas kernels for 0% -> 0%
where the time goes in v1:
time: 171 us; the launch traced here: 170 us
  Pallas kernels  165 us (96%)
  local copies, waits for them, and re-layouts  3.31 us (2%)
  between operations  2.38 us (1%)
    pallas_call x1, Pallas kernels, local_step(): pl.pallas_call(functools.partial(step_kernel, classes), out_shape=(jax.Sh...  165 us

profile of v1, /device:TPU:0, one launch (start us, length us, event | category | flops | bytes accessed | tf_op | source)
XLA Modules:
  0.0 170.5 jit_solution(272553832288640843)
XLA Ops:
  0.6 164.8 %gcn_step.1 = (f32[1,1]{1,0:T(1,128)}, f32[128,256]{1,0:T(8,128)}, f32[349,256]{1,0:T(8,128)}) custom-call(bf16[1024,16384]{1,0:T(8,128)(2,1)} %adj.1, bf16[1024,128]{1,0:T(8,128)(2,1)} %x_ref.1, f32[128,256]{1,0:T(8,128)} %w1_ref.1, f32[349,256]{1,0:T(8,128)} %bitcast.6, s32[8,128]{1,0:T(8,128)} %bitcast.7, s32[8,128]{1,0:T(8,128)} %bitcast.8), custom_call_target="tpu_custom_call" | custom-call | tf_op jit(solution)/shard_map/gcn_step/pallas_call | solution.py:496
  166.0 1.6 copy.13
  167.6 1.7 %copy.14 = f32[256,349]{0,1:T(8,128)} copy(f32[256,349]{0,1:T(8,128)} %bitcast.5) | data formatting | bytes 714752

commit v2 on v1

--- a/solution.py
+++ b/solution.py
@@ -13,7 +13,7 @@
 DEVICES = 16
 UNITS = 4
 LANES = 128
-CHUNK = 512
+CHUNK = 1024
 
 
 def dot(a, b):
@@ -75,7 +75,7 @@
     def a_copy(i):
         return pltpu.make_async_copy(adj.at[:, a_cols(order[i])], a_v.at[:, a_cols(order[i])], a_sem.at[i])
 
-    for i in range(DEVICES):
+    for i in range(2):
         a_copy(i).start()
 
     def rows_of(dev, q):
@@ -88,9 +88,9 @@
         gb[uid(me, q), :unit, :fin] = x_ref[q * unit:(q + 1) * unit, :]
 
     barrier = pltpu.get_barrier_semaphore()
-    for i in range(1, DEVICES):
-        pl.semaphore_signal(barrier, inc=1, device_id=((me + i) % DEVICES,), device_id_type=MESH)
-    pl.semaphore_wait(barrier, DEVICES - 1)
+    for dev in [sib] + nbr:
+        pl.semaphore_signal(barrier, inc=1, device_id=(dev,), device_id_type=MESH)
+    pl.semaphore_wait(barrier, 4)
 
     def pick(f, vals):
         return jnp.where(f == 0, vals[0], jnp.where(f == 1, vals[1], vals[2]))
@@ -186,45 +186,49 @@
         hook(-1, None)
 
         def group(i):
-            hop, q, far = (i // 4) % 2, i % 4, i // 8
-
-            @pl.when(far == 0)
-            def _():
-                g.arrive(hop, q)
-
-            @pl.when(far == 1)
+            @pl.when(i < 8)
+            def _():
+                g.arrive(i // 4, i % 4)
+
+            @pl.when(i == 8)
             def _():
                 for j in range(3):
                     g.arrive_last(j)
+
+            @pl.when(i == 9)
+            def _():
+                g.arrive_last(3)
             hook(None, i)
 
             def half(t):
-                @pl.when(t == 1)
+                k = i - t
+                hop, q, far = (k // 4) % 2, k % 4, k // 8
+
+                @pl.when((k >= 0) & (k <= 8))
                 def _():
-                    @pl.when(far == 0)
+                    @pl.when((t == 1) & (k < 8))
                     def _():
                         g.sib_wait(hop, q)
 
-                    @pl.when(far == 1)
+                    @pl.when((t == 1) & (k == 8))
                     def _():
                         for j in range(3):
                             g.sib_wait_last(j)
-                if first:
-                    for k, (lo, hi) in {(0, 0): (2, 5), (0, 1): (5, 8), (4, 0): (8, 11), (4, 1): (11, 14),
-                                        (8, 0): (14, 15), (8, 1): (15, 16)}.items():
-                        @pl.when((i == k[0]) & (t == k[1]))
-                        def _(lo=lo, hi=hi):
-                            a_wait(lo, hi)
-                pairs = []
-                for r in range(3):
-                    o, s = src_dev(me, own_d, hop, r), src_dev(sib, sib_d, hop, r)
-                    near_dev = o + t * (s - o)
-                    far_dev = anti + t * (anti_sib - anti)
-                    pairs.append((near_dev + far * (far_dev - near_dev), q + far * (r - q)))
-                add(pairs)
+                    if first:
+                        for key, (lo, hi) in {(0, 0): (2, 5), (0, 1): (5, 8), (4, 0): (8, 11), (4, 1): (11, 14),
+                                              (8, 0): (14, 15), (8, 1): (15, 16)}.items():
+                            @pl.when((k == key[0]) & (t == key[1]))
+                            def _(lo=lo, hi=hi):
+                                a_wait(lo, hi)
+                    pairs = []
+                    for r in range(3):
+                        o, s = src_dev(me, own_d, hop, r), src_dev(sib, sib_d, hop, r)
+                        near_dev = o + t * (s - o)
+                        far_dev = anti + t * (anti_sib - anti)
+                        pairs.append((near_dev + far * (far_dev - near_dev), q + far * (r - q)))
+                    add(pairs)
             loop(2, half)
-        loop(9, group)
-        g.arrive_last(3)
+        loop(10, group)
         g.sib_wait_last(3)
 
         def last(m):
@@ -246,6 +250,8 @@
 
     for q in range(UNITS):
         gx.start_own(q)
+    for i in range(2, 8):
+        a_copy(i).start()
     w1b[...] = w1_ref[...].astype(BF16)
     w2acc[...] = jnp.zeros_like(w2acc)
     w2acc[:classes, :] = w2_ref[...]
@@ -263,6 +269,8 @@
     def hook1(pre, i):
         if i is None:
             cnt_copy(0).start()
+            for j in range(8, DEVICES):
+                a_copy(j).start()
             return
         for k in range(4):
             @pl.when(i == k + 1)

time: 171 us -> 165 us (0.965)
  Pallas kernels: 165 us -> 159 us
    pallas_call x1, Pallas kernels: 165 us -> 159 us  [local_step(): pl.pallas_call(functools.partial(step_kernel, classes), out_shape=(jax.Sh...]
where the time goes in v2:
time: 165 us; the launch traced here: 164 us
  Pallas kernels  159 us (96%)
  local copies, waits for them, and re-layouts  3.31 us (2%)
  between operations  2.38 us (1%)
    pallas_call x1, Pallas kernels, local_step(): pl.pallas_call(functools.partial(step_kernel, classes), out_shape=(jax.Sh...  159 us
    unnamed x2, local copies, waits for them, and re-layouts  3.31 us

profile of v2, /device:TPU:0, one launch (start us, length us, event | category | flops | bytes accessed | tf_op | source)
XLA Modules:
  0.0 164.4 jit_solution(1826987586106083991)
XLA Ops:
  0.6 158.7 %gcn_step.1 = (f32[1,1]{1,0:T(1,128)}, f32[128,256]{1,0:T(8,128)}, f32[349,256]{1,0:T(8,128)}) custom-call(bf16[1024,16384]{1,0:T(8,128)(2,1)} %adj.1, bf16[1024,128]{1,0:T(8,128)(2,1)} %x_ref.1, f32[128,256]{1,0:T(8,128)} %w1_ref.1, f32[349,256]{1,0:T(8,128)} %bitcast.6, s32[8,128]{1,0:T(8,128)} %bitcast.7, s32[8,128]{1,0:T(8,128)} %bitcast.8), custom_call_target="tpu_custom_call" | custom-call | tf_op jit(solution)/shard_map/gcn_step/pallas_call | solution.py:504
  159.9 1.6 copy.13
  161.5 1.7 %copy.14 = f32[256,349]{0,1:T(8,128)} copy(f32[256,349]{0,1:T(8,128)} %bitcast.5) | data formatting | bytes 714752

commit v3 on v2

--- a/solution.py
+++ b/solution.py
@@ -35,7 +35,7 @@
 def step_kernel(classes, adj, x_ref, w1_ref, w2_ref, lab_ref, msk_ref,
                 loss_out, g1_out, g2_out,
                 a_v, gb, hb, acc1, acc2, ys1, ys2, hown, e2own, w1b, w2b,
-                w2acc, w2rcv, w2f, w1p, w1r, w1f, cnt_src, cnt_rcv, loss_acc,
+                w2acc, w2rcv, w2part, w2f, w1p, w1r, w1f, cnt_own, cnt_rcv, cnt, loss_acc,
                 a_sem, rsem, ssem, sib_rsem, sib_ssem, cs_sem, cr_sem,
                 w2s_sem, w2r_sem, w1s_sem, w1r_sem, w1gs_sem, w1gr_sem):
     rows = x_ref.shape[0]
@@ -257,33 +257,17 @@
     w2acc[:classes, :] = w2_ref[...]
     w2b[...] = w2acc[:cpad, :].astype(BF16)
 
-    partners = [sib] + nbr
-
     def cnt_copy(i):
-        return remote(cnt_src.at[i], cnt_rcv.at[i], cs_sem.at[i], cr_sem.at[i], partners[i])
+        return remote(cnt_own, cnt_rcv.at[i], cs_sem.at[i], cr_sem.at[i], (me + i) % DEVICES)
 
     local = jnp.sum(msk_ref[...].astype(F32), axis=1, keepdims=True)
     local = jnp.sum(local, axis=0, keepdims=True)
-    cnt_src[0] = jnp.broadcast_to(local, (8, LANES))
+    cnt_own[...] = jnp.broadcast_to(local, (8, LANES))
 
     def hook1(pre, i):
         if i is None:
-            cnt_copy(0).start()
             for j in range(8, DEVICES):
                 a_copy(j).start()
-            return
-        for k in range(4):
-            @pl.when(i == k + 1)
-            def _(k=k):
-                cnt_copy(k).wait_recv()
-                cnt_src[k + 1] = cnt_src[k] + cnt_rcv[k]
-                if k < 3:
-                    cnt_copy(k + 1).start()
-
-        @pl.when(i == 7)
-        def _():
-            for k in range(4):
-                cnt_copy(k).wait_send()
 
     def zero1():
         acc1[...] = jnp.zeros_like(acc1)
@@ -344,7 +328,23 @@
         add_cols(acc2, pairs, lambda j: ys2[j])
 
     loss_acc[...] = jnp.zeros_like(loss_acc)
-    count = cnt_src[4][0:1, :]
+
+    def hook2(pre, i):
+        if i is None:
+            for j in range(1, DEVICES):
+                cnt_copy(j).start()
+            return
+
+        @pl.when(i == 9)
+        def _():
+            for j in range(1, DEVICES):
+                cnt_copy(j).wait_recv()
+            total = cnt_own[...]
+            for j in range(1, DEVICES):
+                total = total + cnt_rcv[j]
+            cnt[...] = total
+            for j in range(1, DEVICES):
+                cnt_copy(j).wait_send()
 
     def finish2(m, pairs):
         s = mrows(m)
@@ -369,11 +369,11 @@
             mask = msk_ref[pl.ds(which, 1), :].astype(F32)
             picked = jnp.sum(jnp.where(hot, zc, 0.0), axis=0, keepdims=True)
             loss_acc[...] = loss_acc[...] + mask * (log_norm - picked)
-            gr = (jnp.exp(zm - log_norm) - jnp.where(hot, 1.0, 0.0)) * (mask / count)
+            gr = (jnp.exp(zm - log_norm) - jnp.where(hot, 1.0, 0.0)) * (mask / cnt[0:1, :])
             gb[uid(me, m), :, h * LANES:(h + 1) * LANES] = gr.astype(BF16)
         gg.start_own(m)
 
-    phase(gh, add2, zero2, finish2, lambda pre, i: None, False)
+    phase(gh, add2, zero2, finish2, hook2, False)
 
     def finish3(m, pairs):
         s = mrows(m)
@@ -390,27 +390,33 @@
           lambda pre, i: None, False)
 
     total_rows = w2acc.shape[0]
-    size = [total_rows // 2, total_rows // 4, total_rows // 8, total_rows // 16]
-    bits = [core] + role_bit
-    base = [0]
-    for i in range(4):
-        base.append(base[i] + bits[i] * size[i])
-    roff = [0, size[0], size[0] + size[1], size[0] + size[1] + size[2]]
+    half_rows = total_rows // 2
+    piece = half_rows // 8
+    chips = DEVICES // 2
+    chip = me // 2
 
     def w2rows(start, n):
         return pl.ds(pl.multiple_of(start, 8), n)
 
-    def w2_scatter(i):
-        out = w2acc.at[w2rows(base[i] + (1 - bits[i]) * size[i], size[i])]
-        return remote(out, w2rcv.at[pl.ds(roff[i], size[i])], w2s_sem.at[i], w2r_sem.at[i], partners[i])
-
-    def w2_gather(i):
-        out = w2f.at[w2rows(base[i + 1], size[i])]
-        return remote(out, out, w2s_sem.at[4 + i], w2r_sem.at[4 + i], partners[i])
-
-    def w2_gather_in(i):
-        out = w2f.at[w2rows(base[i] + (1 - bits[i]) * size[i], size[i])]
-        return remote(out, out, w2s_sem.at[4 + i], w2r_sem.at[4 + i], partners[i])
+    mine = w2rows(core * half_rows, half_rows)
+
+    def w2_sib():
+        out = w2acc.at[w2rows((1 - core) * half_rows, half_rows)]
+        return remote(out, w2rcv, w2s_sem.at[0], w2r_sem.at[0], sib)
+
+    def w2_scatter(j):
+        to = (chip + j) % chips
+        out = w2acc.at[w2rows(core * half_rows + to * piece, piece)]
+        return remote(out, w2part.at[j], w2s_sem.at[j], w2r_sem.at[j], to * 2 + core)
+
+    def w2_gather(j, frm):
+        to = (chip + j) % chips
+        out = w2f.at[w2rows(core * half_rows + frm * piece, piece)]
+        return remote(out, out, w2s_sem.at[chips + j], w2r_sem.at[chips + j], to * 2 + core)
+
+    def w2_sib_gather(c):
+        out = w2f.at[w2rows(c * half_rows, half_rows)]
+        return remote(out, out, w2s_sem.at[chips], w2r_sem.at[chips], sib)
 
     def hook4(pre, i):
         if i is None:
@@ -421,22 +427,35 @@
 
         @pl.when(i == 0)
         def _():
-            w2_scatter(0).start()
-        for k in range(4):
-            @pl.when(i == k + 1)
-            def _(k=k):
-                w2_scatter(k).wait_recv()
-                mine = w2rows(base[k + 1], size[k])
-                into = w2acc if k < 3 else w2f
-                into[mine, :] = w2acc[mine, :] + w2rcv[roff[k]:roff[k] + size[k], :]
-                w2_scatter(k).wait_send()
-                (w2_scatter(k + 1) if k < 3 else w2_gather(3)).start()
-        for k in range(3):
-            @pl.when(i == k + 5)
-            def _(j=3 - k):
-                w2_gather_in(j).wait_recv()
-                w2_gather(j).wait_send()
-                w2_gather(j - 1).start()
+            w2_sib().start()
+
+        @pl.when(i == 1)
+        def _():
+            w2_sib().wait_recv()
+            w2acc[mine, :] = w2acc[mine, :] + w2rcv[...]
+
+        @pl.when(i == 2)
+        def _():
+            w2_sib().wait_send()
+            for j in range(1, chips):
+                w2_scatter(j).start()
+
+        @pl.when(i == 8)
+        def _():
+            own = w2rows(core * half_rows + chip * piece, piece)
+            total = w2acc[own, :]
+            for j in range(1, chips):
+                w2_scatter(j).wait_recv()
+            for j in range(1, chips):
+                total = total + w2part[j]
+            w2f[own, :] = total
+            for j in range(1, chips):
+                w2_scatter(j).wait_send()
+
+        @pl.when(i == 9)
+        def _():
+            for j in range(1, chips):
+                w2_gather(j, chip).start()
 
     def finish4(m, pairs):
         s = mrows(m)
@@ -468,11 +487,12 @@
 
     for i in range(1, DEVICES):
         w1_scatter(i).start()
-    w2_gather_in(0).wait_recv()
-    w2_gather(0).wait_send()
-    g2_out[...] = w2f[:classes, :]
-    loss_out[0, 0] = jnp.sum(w2f[total_rows - 1:, :LANES] / cnt_src[4][0:1, :])
     total = w1p[w1rows(me), :]
+    for j in range(1, chips):
+        w2_gather(j, (chip + chips - j) % chips).wait_recv()
+    w2_sib_gather(core).start()
+    for j in range(1, chips):
+        w2_gather(j, chip).wait_send()
     for i in range(1, DEVICES):
         w1_scatter(i).wait_recv()
     for i in range(1, DEVICES):
@@ -482,6 +502,10 @@
         w1_scatter(i).wait_send()
     for i in range(1, DEVICES):
         w1_gather(i).start()
+    w2_sib_gather(1 - core).wait_recv()
+    w2_sib_gather(core).wait_send()
+    g2_out[...] = w2f[:classes, :]
+    loss_out[0, 0] = jnp.sum(w2f[total_rows - 1:, :LANES] / cnt[0:1, :])
     for i in range(1, DEVICES):
         w1_gather_in(i).wait_recv()
     g1_out[...] = w1f[...]
@@ -521,17 +545,19 @@
                 pltpu.VMEM((fin, hid), BF16),
                 pltpu.VMEM((cpad, hid), BF16),
                 pltpu.VMEM((total_rows, hid), F32),
-                pltpu.VMEM((total_rows, hid), F32),
+                pltpu.VMEM((total_rows // 2, hid), F32),
+                pltpu.VMEM((8, total_rows // 16, hid), F32),
                 pltpu.VMEM((total_rows, hid), F32),
                 pltpu.VMEM((fin, hid), F32),
                 pltpu.VMEM((DEVICES, fin // DEVICES, hid), F32),
                 pltpu.VMEM((fin, hid), F32),
-                pltpu.VMEM((5, 8, LANES), F32),
-                pltpu.VMEM((4, 8, LANES), F32),
+                pltpu.VMEM((8, LANES), F32),
+                pltpu.VMEM((DEVICES, 8, LANES), F32),
+                pltpu.VMEM((8, LANES), F32),
                 pltpu.VMEM((1, LANES), F32),
                 dma((DEVICES,)),
                 dma((2, 28)), dma((2, 28)), dma((2, 32)), dma((2, 32)),
-                dma((4,)), dma((4,)), dma((8,)), dma((8,)),
+                dma((DEVICES,)), dma((DEVICES,)), dma((DEVICES,)), dma((DEVICES,)),
                 dma((DEVICES,)), dma((DEVICES,)), dma((DEVICES,)), dma((DEVICES,)),
             ],
             compiler_params=pltpu.CompilerParams(collective_id=0, has_side_effects=True,

time: 165 us -> 152 us (0.921)
  Pallas kernels: 159 us -> 146 us
    pallas_call x1, Pallas kernels: 159 us -> 146 us  [local_step(): pl.pallas_call(functools.partial(step_kernel, classes), out_shape=(jax.Sh...]
where the time goes in v3:
time: 152 us
  Pallas kernels  146 us (96%)
  local copies, waits for them, and re-layouts  3.31 us (2%)
  between operations  2.38 us (2%)
    pallas_call x1, Pallas kernels, local_step(): pl.pallas_call(functools.partial(step_kernel, classes), out_shape=(jax.Sh...  146 us
    unnamed x2, local copies, waits for them, and re-layouts  3.31 us

profile of v3, /device:TPU:0, one launch (start us, length us, event | category | flops | bytes accessed | tf_op | source)
XLA Modules:
  0.0 151.5 jit_solution(6708666522352908960)
XLA Ops:
  0.6 145.8 %gcn_step.1 = (f32[1,1]{1,0:T(1,128)}, f32[128,256]{1,0:T(8,128)}, f32[349,256]{1,0:T(8,128)}) custom-call(bf16[1024,16384]{1,0:T(8,128)(2,1)} %adj.1, bf16[1024,128]{1,0:T(8,128)(2,1)} %x_ref.1, f32[128,256]{1,0:T(8,128)} %w1_ref.1, f32[349,256]{1,0:T(8,128)} %bitcast.6, s32[8,128]{1,0:T(8,128)} %bitcast.7, s32[8,128]{1,0:T(8,128)} %bitcast.8), custom_call_target="tpu_custom_call" | custom-call | tf_op jit(solution)/shard_map/gcn_step/pallas_call | solution.py:528
  147.1 1.6 %copy.13 = f32[128,256]{1,0:T(8,128)} copy(f32[128,256]{1,0:T(8,128)} %get-tuple-element.13) | data formatting | bytes 262144
  148.6 1.7 %copy.14 = f32[256,349]{0,1:T(8,128)} copy(f32[256,349]{0,1:T(8,128)} %bitcast.5) | data formatting | bytes 714752

commit v4 on v3

--- a/solution.py
+++ b/solution.py
@@ -32,8 +32,9 @@
     lax.fori_loop(0, n, lambda i, c: (fn(i), c)[1], 0)
 
 
-def step_kernel(classes, adj, x_ref, w1_ref, w2_ref, lab_ref, msk_ref,
+def step_kernel(classes, adj, x_hbm, w1_hbm, w2_hbm, lab_hbm, msk_hbm,
                 loss_out, g1_out, g2_out,
+                x_ref, w1_ref, w2_ref, lab_ref, msk_ref, in_sem,
                 a_v, gb, hb, acc1, acc2, ys1, ys2, hown, e2own, w1b, w2b,
                 w2acc, w2rcv, w2part, w2f, w1p, w1r, w1f, cnt_own, cnt_rcv, cnt, loss_acc,
                 a_sem, rsem, ssem, sib_rsem, sib_ssem, cs_sem, cr_sem,
@@ -63,6 +64,13 @@
         return pltpu.make_async_remote_copy(src_ref=src, dst_ref=dst, send_sem=ss, recv_sem=rs,
                                             device_id=(dev,), device_id_type=MESH)
 
+    barrier = pltpu.get_barrier_semaphore()
+    for dev in [sib] + nbr:
+        pl.semaphore_signal(barrier, inc=1, device_id=(dev,), device_id_type=MESH)
+
+    def uid(dev, q):
+        return dev * UNITS + q
+
     order = [me, sib]
     for hop in (0, 1):
         order += [src_dev(me, own_d, hop, r) for r in range(3)]
@@ -75,29 +83,26 @@
     def a_copy(i):
         return pltpu.make_async_copy(adj.at[:, a_cols(order[i])], a_v.at[:, a_cols(order[i])], a_sem.at[i])
 
+    x_units = [pltpu.make_async_copy(x_hbm.at[pl.ds(q * unit, unit)], gb.at[uid(me, q), pl.ds(0, unit), pl.ds(0, fin)],
+                                     in_sem.at[q]) for q in range(UNITS)]
+    inputs = [pltpu.make_async_copy(src, dst, in_sem.at[UNITS + i]) for i, (src, dst) in enumerate(
+        [(w1_hbm, w1_ref), (w2_hbm, w2_ref), (msk_hbm, msk_ref), (lab_hbm, lab_ref), (x_hbm, x_ref)])]
+    for c in x_units + inputs:
+        c.start()
     for i in range(2):
         a_copy(i).start()
 
     def rows_of(dev, q):
         return pl.ds(pl.multiple_of(dev * rows + q * unit, unit), unit)
 
-    def uid(dev, q):
-        return dev * UNITS + q
-
-    for q in range(UNITS):
-        gb[uid(me, q), :unit, :fin] = x_ref[q * unit:(q + 1) * unit, :]
-
-    barrier = pltpu.get_barrier_semaphore()
-    for dev in [sib] + nbr:
-        pl.semaphore_signal(barrier, inc=1, device_id=(dev,), device_id_type=MESH)
     pl.semaphore_wait(barrier, 4)
 
     def pick(f, vals):
         return jnp.where(f == 0, vals[0], jnp.where(f == 1, vals[1], vals[2]))
 
     class Gather:
-        def __init__(self, view, par):
-            self.view, self.par = view, par
+        def __init__(self, view, height, par):
+            self.view, self.height, self.par = view, height, par
 
         def hop_copy(self, dev, q, to, sslot, rslot):
             v = self.view(dev, q)
@@ -123,6 +128,19 @@
             dev = pick((to + 2) % 3, [src_dev(me, own_d, 1, r) for r in range(3)])
             return self.hop_copy(dev, q, pick(to, nbr), 24 + q, 24 + q)
 
+        def thirds(self, dev):
+            tiles = self.height // 16
+            at = [0, tiles // 3 * 16, 2 * (tiles // 3) * 16, self.height]
+            return [self.view(dev, 3).at[pl.ds(at[t], at[t + 1] - at[t])] for t in range(3)]
+
+        def third_copy(self, t):
+            v = self.thirds(src_dev(me, own_d, 1, (t + 2) % 3))[t]
+            return remote(v, v, ssem.at[self.par, 27 + t], rsem.at[self.par, 27 + t], nbr[t])
+
+        def third_in(self, t):
+            v = self.thirds(anti)[t]
+            return remote(v, v, ssem.at[self.par, 27 + t], rsem.at[self.par, 27 + t], nbr[t])
+
         def arrive(self, hop, q):
             for r in range(3):
                 d = src_dev(me, own_d, hop, r)
@@ -133,14 +151,23 @@
                 for c in self.forward(q):
                     c.start()
 
-            @pl.when(hop == 1)
+            @pl.when((hop == 1) & (q < 3))
             def _():
                 self.last_forward(q).start()
+
+            @pl.when((hop == 1) & (q == 3))
+            def _():
+                for t in range(3):
+                    self.third_copy(t).start()
             for r in range(3):
                 self.sib_copy(src_dev(me, own_d, hop, r), q, hop * 12 + r * 4 + q).start()
 
         def arrive_last(self, q):
-            self.hop_copy(anti, q, nbr[0], 24 + q, 24 + q).wait_recv()
+            if q < 3:
+                self.hop_copy(anti, q, nbr[0], 24 + q, 24 + q).wait_recv()
+            else:
+                for t in range(3):
+                    self.third_in(t).wait_recv()
             self.sib_copy(anti, q, 24 + q).start()
 
         def sib_wait(self, hop, q):
@@ -155,11 +182,15 @@
 
         def wait_sends(self):
             def body(q):
-                for c in self.own_copies(q) + self.forward(q) + [self.last_forward(q)]:
+                for c in self.own_copies(q) + self.forward(q):
                     c.wait_send()
                 for slot in (q, 4 + q, 8 + q, 12 + q, 16 + q, 20 + q, 24 + q):
                     self.sib_copy(me, q, slot).wait_send()
             loop(UNITS, body)
+            for q in range(3):
+                self.last_forward(q).wait_send()
+            for t in range(3):
+                self.third_copy(t).wait_send()
 
     def phase(g, add, zero, finish, hook, first):
         def a_wait(lo, hi):
@@ -229,18 +260,19 @@
                     add(pairs)
             loop(2, half)
         loop(10, group)
+        add([(anti, 3)])
         g.sib_wait_last(3)
 
         def last(m):
             @pl.when(m == UNITS - 1)
             def _():
                 g.wait_sends()
-            finish(m, [(anti, 3), (anti_sib, 3)])
+            finish(m, [(anti_sib, 3)])
         loop(UNITS, last)
 
-    gx = Gather(lambda dev, q: gb.at[uid(dev, q), pl.ds(0, unit), pl.ds(0, fin)], 0)
-    gh = Gather(lambda dev, q: hb.at[rows_of(dev, q)], 1)
-    gg = Gather(lambda dev, q: gb.at[uid(dev, q)], 0)
+    gx = Gather(lambda dev, q: gb.at[uid(dev, q), pl.ds(0, unit), pl.ds(0, fin)], unit, 0)
+    gh = Gather(lambda dev, q: hb.at[rows_of(dev, q)], unit, 1)
+    gg = Gather(lambda dev, q: gb.at[uid(dev, q)], cpad, 0)
 
     def mrows(m):
         return pl.ds(pl.multiple_of(m * unit, unit), unit)
@@ -249,9 +281,12 @@
         return pl.ds(pl.multiple_of(c * CHUNK, CHUNK), CHUNK)
 
     for q in range(UNITS):
+        x_units[q].wait()
         gx.start_own(q)
     for i in range(2, 8):
         a_copy(i).start()
+    for c in inputs:
+        c.wait()
     w1b[...] = w1_ref[...].astype(BF16)
     w2acc[...] = jnp.zeros_like(w2acc)
     w2acc[:classes, :] = w2_ref[...]
@@ -530,9 +565,15 @@
             out_shape=(jax.ShapeDtypeStruct((1, 1), F32),
                        jax.ShapeDtypeStruct((fin, hid), F32),
                        jax.ShapeDtypeStruct((classes, hid), F32)),
-            in_specs=[pl.BlockSpec(memory_space=pl.ANY)] + [vm] * 5,
+            in_specs=[pl.BlockSpec(memory_space=pl.ANY)] * 6,
             out_specs=(pl.BlockSpec(memory_space=pltpu.SMEM), vm, vm),
             scratch_shapes=[
+                pltpu.VMEM((rows, fin), BF16),
+                pltpu.VMEM((fin, hid), F32),
+                pltpu.VMEM((classes, hid), F32),
+                pltpu.VMEM((rows // LANES, LANES), jnp.int32),
+                pltpu.VMEM((rows // LANES, LANES), jnp.int32),
+                dma((UNITS + 5,)),
                 pltpu.VMEM((rows, nodes), BF16),
                 pltpu.VMEM((nodes // unit, cpad, unit), BF16),
                 pltpu.VMEM((nodes, hid), BF16),
@@ -556,7 +597,7 @@
                 pltpu.VMEM((8, LANES), F32),
                 pltpu.VMEM((1, LANES), F32),
                 dma((DEVICES,)),
-                dma((2, 28)), dma((2, 28)), dma((2, 32)), dma((2, 32)),
+                dma((2, 30)), dma((2, 30)), dma((2, 32)), dma((2, 32)),
                 dma((DEVICES,)), dma((DEVICES,)), dma((DEVICES,)), dma((DEVICES,)),
                 dma((DEVICES,)), dma((DEVICES,)), dma((DEVICES,)), dma((DEVICES,)),
             ],

time: 152 us -> 151 us (level)
  no operation moved by 1% of the time
where the time goes in v4:
time: 151 us
  Pallas kernels  145 us (96%)
  local copies, waits for them, and re-layouts  3.31 us (2%)
  between operations  2.38 us (2%)
    pallas_call x1, Pallas kernels, local_step(): pl.pallas_call(functools.partial(step_kernel, classes), out_shape=(jax.Sh...  145 us
    unnamed x2, local copies, waits for them, and re-layouts  3.31 us

profile of v4, /device:TPU:0, one launch (start us, length us, event | category | flops | bytes accessed | tf_op | source)
XLA Modules:
  0.0 150.9 jit_solution(15542471308365300304)
XLA Ops:
  0.6 145.2 %gcn_step.1 = (f32[1,1]{1,0:T(1,128)}, f32[128,256]{1,0:T(8,128)}, f32[349,256]{1,0:T(8,128)}) custom-call(bf16[1024,16384]{1,0:T(8,128)(2,1)} %adj.1, bf16[1024,128]{1,0:T(8,128)(2,1)} %x_hbm.1, f32[128,256]{1,0:T(8,128)} %w1_hbm.1, f32[349,256]{1,0:T(8,128)} %bitcast.6, s32[8,128]{1,0:T(8,128)} %bitcast.7, s32[8,128]{1,0:T(8,128)} %bitcast.8), custom_call_target="tpu_custom_call" | custom-call | tf_op jit(solution)/shard_map/gcn_step/pallas_call | solution.py:563
  146.4 1.6 %copy.13 = f32[128,256]{1,0:T(8,128)} copy(f32[128,256]{1,0:T(8,128)} %get-tuple-element.13) | data formatting | bytes 262144
  148.0 1.7 %copy.14 = f32[256,349]{0,1:T(8,128)} copy(f32[256,349]{0,1:T(8,128)} %bitcast.5) | data formatting | bytes 714752

commit v5 on v4

--- a/solution.py
+++ b/solution.py
@@ -101,19 +101,21 @@
         return jnp.where(f == 0, vals[0], jnp.where(f == 1, vals[1], vals[2]))
 
     class Gather:
-        def __init__(self, view, height, par):
+        def __init__(self, view, height, par, sib_view=None):
             self.view, self.height, self.par = view, height, par
+            self.shared, self.sib_view = sib_view is not None, sib_view or view
 
         def hop_copy(self, dev, q, to, sslot, rslot):
             v = self.view(dev, q)
             return remote(v, v, ssem.at[self.par, sslot], rsem.at[self.par, rslot], to)
 
-        def sib_copy(self, dev, q, slot):
-            v = self.view(dev, q)
-            return remote(v, v, sib_ssem.at[self.par, slot], sib_rsem.at[self.par, slot], sib)
+        def sib_copy(self, dev, q, slot, src=None):
+            v = self.sib_view(dev, q)
+            return remote(v if src is None else src, v, sib_ssem.at[self.par, slot], sib_rsem.at[self.par, slot], sib)
 
         def own_copies(self, q):
-            return [self.hop_copy(me, q, nbr[r], r * 4 + q, r * 4 + q) for r in range(3)] + [self.sib_copy(me, q, 28 + q)]
+            hops = [self.hop_copy(me, q, nbr[r], r * 4 + q, r * 4 + q) for r in range(3)]
+            return hops if self.shared else hops + [self.sib_copy(me, q, 28 + q)]
 
         def start_own(self, q):
             for c in self.own_copies(q):
@@ -159,8 +161,9 @@
             def _():
                 for t in range(3):
                     self.third_copy(t).start()
-            for r in range(3):
-                self.sib_copy(src_dev(me, own_d, hop, r), q, hop * 12 + r * 4 + q).start()
+            if not self.shared:
+                for r in range(3):
+                    self.sib_copy(src_dev(me, own_d, hop, r), q, hop * 12 + r * 4 + q).start()
 
         def arrive_last(self, q):
             if q < 3:
@@ -168,7 +171,8 @@
             else:
                 for t in range(3):
                     self.third_in(t).wait_recv()
-            self.sib_copy(anti, q, 24 + q).start()
+            if not self.shared:
+                self.sib_copy(anti, q, 24 + q).start()
 
         def sib_wait(self, hop, q):
             for r in range(3):
@@ -184,9 +188,13 @@
             def body(q):
                 for c in self.own_copies(q) + self.forward(q):
                     c.wait_send()
-                for slot in (q, 4 + q, 8 + q, 12 + q, 16 + q, 20 + q, 24 + q):
-                    self.sib_copy(me, q, slot).wait_send()
+                if not self.shared:
+                    for slot in (q, 4 + q, 8 + q, 12 + q, 16 + q, 20 + q, 24 + q):
+                        self.sib_copy(me, q, slot).wait_send()
             loop(UNITS, body)
+            if self.shared:
+                for slot in (15, 19, 23, 24, 25, 26, 27, 28, 29, 30, 31):
+                    self.sib_copy(me, 0, slot).wait_send()
             for q in range(3):
                 self.last_forward(q).wait_send()
             for t in range(3):
@@ -200,20 +208,28 @@
 
         zero()
 
+        def halves(fn):
+            if g.shared:
+                fn(0)
+                fn(1)
+            else:
+                loop(2, fn)
+
         def near(t):
-            if first:
-                @pl.when(t == 0)
-                def _():
-                    a_wait(0, 1)
-
-            @pl.when(t == 1)
-            def _():
+            if first and t == 0:
+                a_wait(0, 1)
+
+            def wait_sib():
                 for q in range(UNITS):
                     g.sib_wait_own(q)
                 a_wait(1, 2)
+            if not g.shared:
+                pl.when(t == 1)(wait_sib)
+            elif t == 1:
+                wait_sib()
             dev = me + t * (sib - me)
-            add([(dev, q) for q in range(UNITS)])
-        loop(2, near)
+            add([(dev, q) for q in range(UNITS)], t, -1)
+        halves(near)
         hook(-1, None)
 
         def group(i):
@@ -237,30 +253,31 @@
 
                 @pl.when((k >= 0) & (k <= 8))
                 def _():
-                    @pl.when((t == 1) & (k < 8))
-                    def _():
-                        g.sib_wait(hop, q)
-
-                    @pl.when((t == 1) & (k == 8))
-                    def _():
-                        for j in range(3):
-                            g.sib_wait_last(j)
+                    def on_sib(cond, fn):
+                        if not g.shared:
+                            pl.when((t == 1) & cond)(fn)
+                        elif t == 1:
+                            pl.when(cond)(fn)
+
+                    on_sib(k < 8, lambda: g.sib_wait(hop, q))
+                    on_sib(k == 8, lambda: [g.sib_wait_last(j) for j in range(3)] and None)
                     if first:
                         for key, (lo, hi) in {(0, 0): (2, 5), (0, 1): (5, 8), (4, 0): (8, 11), (4, 1): (11, 14),
                                               (8, 0): (14, 15), (8, 1): (15, 16)}.items():
-                            @pl.when((k == key[0]) & (t == key[1]))
-                            def _(lo=lo, hi=hi):
-                                a_wait(lo, hi)
+                            if t == key[1]:
+                                @pl.when(k == key[0])
+                                def _(lo=lo, hi=hi):
+                                    a_wait(lo, hi)
                     pairs = []
                     for r in range(3):
                         o, s = src_dev(me, own_d, hop, r), src_dev(sib, sib_d, hop, r)
                         near_dev = o + t * (s - o)
                         far_dev = anti + t * (anti_sib - anti)
                         pairs.append((near_dev + far * (far_dev - near_dev), q + far * (r - q)))
-                    add(pairs)
-            loop(2, half)
+                    add(pairs, t, k)
+            halves(half)
         loop(10, group)
-        add([(anti, 3)])
+        add([(anti, 3)], 0, 9)
         g.sib_wait_last(3)
 
         def last(m):
@@ -270,7 +287,8 @@
             finish(m, [(anti_sib, 3)])
         loop(UNITS, last)
 
-    gx = Gather(lambda dev, q: gb.at[uid(dev, q), pl.ds(0, unit), pl.ds(0, fin)], unit, 0)
+    gx = Gather(lambda dev, q: gb.at[uid(dev, q), pl.ds(0, unit), pl.ds(0, fin)], unit, 0,
+                lambda dev, q: gb.at[uid(dev, q), pl.ds(0, unit), pl.ds(0, hid)])
     gh = Gather(lambda dev, q: hb.at[rows_of(dev, q)], unit, 1)
     gg = Gather(lambda dev, q: gb.at[uid(dev, q)], cpad, 0)
 
@@ -307,9 +325,6 @@
     def zero1():
         acc1[...] = jnp.zeros_like(acc1)
 
-    def y1(dev, q):
-        return dot(gb[uid(dev, q), :unit, :fin], w1b[...]).astype(BF16)
-
     def add_rows(acc, pairs, operand):
         def body(c):
             s = chunk(c)
@@ -319,21 +334,41 @@
             acc[s, :] = v
         loop(rows // CHUNK, body)
 
-    def add1(pairs):
+    def add1(pairs, t, k):
+        if t == 1:
+            add_rows(acc1, pairs, lambda j: gb[uid(*pairs[j]), :unit, :hid])
+            return
+        n = len(pairs)
+        if isinstance(k, int):
+            at = 0 if k < 0 else 10
+            slots = [28 + j for j in range(n)] if k < 0 else [27]
+        else:
+            hop, q, far = (k // 4) % 2, k % 4, k // 8
+            at = UNITS + 3 * (k % 2)
+            slots = [hop * 12 + r * 4 + q + far * (24 + r - hop * 12 - r * 4 - q) for r in range(3)]
+
+            @pl.when(k >= 2)
+            def _():
+                back = k - 2
+                for r in range(3):
+                    gx.sib_copy(me, 0, (back // 4) * 12 + r * 4 + back % 4).wait_send()
         for j, (dev, q) in enumerate(pairs):
-            ys1[j] = y1(dev, q)
-        add_rows(acc1, pairs, lambda j: ys1[j])
+            ys1[at + j] = dot(gb[uid(dev, q), :unit, :fin], w1b[...]).astype(BF16)
+
+        def send():
+            for j, (dev, q) in enumerate(pairs):
+                gx.sib_copy(dev, q, slots[j], ys1.at[at + j]).start()
+        if isinstance(k, int):
+            send()
+        add_rows(acc1, pairs, lambda j: ys1[at + j])
+        if not isinstance(k, int):
+            send()
 
     def finish1(m, pairs):
         s = mrows(m)
-
-        @pl.when(m == 0)
-        def _():
-            for j, (dev, q) in enumerate(pairs):
-                ys1[j] = y1(dev, q)
         z = acc1[s, :]
-        for j, (dev, q) in enumerate(pairs):
-            z = z + dot(a_v[s, rows_of(dev, q)], ys1[j])
+        for dev, q in pairs:
+            z = z + dot(a_v[s, rows_of(dev, q)], gb[uid(dev, q), :unit, :hid])
         acc1[s, :] = z
         h = jnp.maximum(z, 0.0).astype(BF16)
         hb[rows_of(me, m), :] = h
@@ -357,7 +392,7 @@
             acc[:, s] = v
         loop(rows // CHUNK, body)
 
-    def add2(pairs):
+    def add2(pairs, t, k):
         for j, (dev, q) in enumerate(pairs):
             ys2[j] = y2(dev, q)
         add_cols(acc2, pairs, lambda j: ys2[j])
@@ -421,7 +456,7 @@
         hb[rows_of(me, m), :] = jnp.where(acc1[s, :] > 0.0, gz, 0.0).astype(BF16)
         gh.start_own(m)
 
-    phase(gg, lambda pairs: add_cols(acc2, pairs, lambda j: gb[uid(*pairs[j])]), zero2, finish3,
+    phase(gg, lambda pairs, t, k: add_cols(acc2, pairs, lambda j: gb[uid(*pairs[j])]), zero2, finish3,
           lambda pre, i: None, False)
 
     total_rows = w2acc.shape[0]
@@ -469,28 +504,11 @@
             w2_sib().wait_recv()
             w2acc[mine, :] = w2acc[mine, :] + w2rcv[...]
 
-        @pl.when(i == 2)
+        @pl.when(i == 9)
         def _():
             w2_sib().wait_send()
             for j in range(1, chips):
                 w2_scatter(j).start()
-
-        @pl.when(i == 8)
-        def _():
-            own = w2rows(core * half_rows + chip * piece, piece)
-            total = w2acc[own, :]
-            for j in range(1, chips):
-                w2_scatter(j).wait_recv()
-            for j in range(1, chips):
-                total = total + w2part[j]
-            w2f[own, :] = total
-            for j in range(1, chips):
-                w2_scatter(j).wait_send()
-
-        @pl.when(i == 9)
-        def _():
-            for j in range(1, chips):
-                w2_gather(j, chip).start()
 
     def finish4(m, pairs):
         s = mrows(m)
@@ -501,7 +519,7 @@
         w1p[...] = w1p[...] + part
 
     w1p[...] = jnp.zeros_like(w1p)
-    phase(gh, lambda pairs: add_rows(acc1, pairs, lambda j: hb[rows_of(*pairs[j]), :]), zero1, finish4, hook4, False)
+    phase(gh, lambda pairs, t, k: add_rows(acc1, pairs, lambda j: hb[rows_of(*pairs[j]), :]), zero1, finish4, hook4, False)
 
     sl = fin // DEVICES
 
@@ -522,12 +540,18 @@
 
     for i in range(1, DEVICES):
         w1_scatter(i).start()
+    own = w2rows(core * half_rows + chip * piece, piece)
+    total2 = w2acc[own, :]
+    for j in range(1, chips):
+        w2_scatter(j).wait_recv()
+    for j in range(1, chips):
+        total2 = total2 + w2part[j]
+    w2f[own, :] = total2
+    for j in range(1, chips):
+        w2_scatter(j).wait_send()
+    for j in range(1, chips):
+        w2_gather(j, chip).start()
     total = w1p[w1rows(me), :]
-    for j in range(1, chips):
-        w2_gather(j, (chip + chips - j) % chips).wait_recv()
-    w2_sib_gather(core).start()
-    for j in range(1, chips):
-        w2_gather(j, chip).wait_send()
     for i in range(1, DEVICES):
         w1_scatter(i).wait_recv()
     for i in range(1, DEVICES):
@@ -537,13 +561,18 @@
         w1_scatter(i).wait_send()
     for i in range(1, DEVICES):
         w1_gather(i).start()
+    for j in range(1, chips):
+        w2_gather(j, (chip + chips - j) % chips).wait_recv()
+    w2_sib_gather(core).start()
+    for j in range(1, chips):
+        w2_gather(j, chip).wait_send()
     w2_sib_gather(1 - core).wait_recv()
-    w2_sib_gather(core).wait_send()
     g2_out[...] = w2f[:classes, :]
     loss_out[0, 0] = jnp.sum(w2f[total_rows - 1:, :LANES] / cnt[0:1, :])
     for i in range(1, DEVICES):
         w1_gather_in(i).wait_recv()
     g1_out[...] = w1f[...]
+    w2_sib_gather(core).wait_send()
     for i in range(1, DEVICES):
         w1_gather(i).wait_send()
 
@@ -579,7 +608,7 @@
                 pltpu.VMEM((nodes, hid), BF16),
                 pltpu.VMEM((rows, hid), F32),
                 pltpu.VMEM((cpad, rows), F32),
-                pltpu.VMEM((UNITS, unit, hid), BF16),
+                pltpu.VMEM((UNITS + 7, unit, hid), BF16),
                 pltpu.VMEM((UNITS, cpad, unit), BF16),
                 pltpu.VMEM((rows, hid), BF16),
                 pltpu.VMEM((cpad, rows), BF16),

time: 151 us -> 149 us (0.987)
  Pallas kernels: 145 us -> 143 us
    pallas_call x1, Pallas kernels: 145 us -> 143 us  [local_step(): pl.pallas_call(functools.partial(step_kernel, classes), out_shape=(jax.Sh...]
where the time goes in v5:
time: 149 us
  Pallas kernels  143 us (96%)
  local copies, waits for them, and re-layouts  3.31 us (2%)
  between operations  2.38 us (2%)
    pallas_call x1, Pallas kernels, local_step(): pl.pallas_call(functools.partial(step_kernel, classes), out_shape=(jax.Sh...  143 us
    unnamed x2, local copies, waits for them, and re-layouts  3.31 us

profile of v5, /device:TPU:0, one launch (start us, length us, event | category | flops | bytes accessed | tf_op | source)
XLA Modules:
  0.0 149.0 jit_solution(14085158988151869864)
XLA Ops:
  0.6 143.3 %gcn_step.1 = (f32[1,1]{1,0:T(1,128)}, f32[128,256]{1,0:T(8,128)}, f32[349,256]{1,0:T(8,128)}) custom-call(bf16[1024,16384]{1,0:T(8,128)(2,1)} %adj.1, bf16[1024,128]{1,0:T(8,128)(2,1)} %x_hbm.1, f32[128,256]{1,0:T(8,128)} %w1_hbm.1, f32[349,256]{1,0:T(8,128)} %bitcast.6, s32[8,128]{1,0:T(8,128)} %bitcast.7, s32[8,128]{1,0:T(8,128)} %bitcast.8), custom_call_target="tpu_custom_call" | custom-call | tf_op jit(solution)/shard_map/gcn_step/pallas_call | solution.py:592
  144.5 1.6 %copy.13 = f32[128,256]{1,0:T(8,128)} copy(f32[128,256]{1,0:T(8,128)} %get-tuple-element.13) | data formatting | bytes 262144
  146.1 1.7 %copy.14 = f32[256,349]{0,1:T(8,128)} copy(f32[256,349]{0,1:T(8,128)} %bitcast.5) | data formatting | bytes 714752

commit v6 on v5

--- a/solution.py
+++ b/solution.py
@@ -36,7 +36,7 @@
                 loss_out, g1_out, g2_out,
                 x_ref, w1_ref, w2_ref, lab_ref, msk_ref, in_sem,
                 a_v, gb, hb, acc1, acc2, ys1, ys2, hown, e2own, w1b, w2b,
-                w2acc, w2rcv, w2part, w2f, w1p, w1r, w1f, cnt_own, cnt_rcv, cnt, loss_acc,
+                w2acc, w2rcv, w2part, w2f, w1p, w1r, w1f, cnt_src, cnt_rcv, loss_acc, xt,
                 a_sem, rsem, ssem, sib_rsem, sib_ssem, cs_sem, cr_sem,
                 w2s_sem, w2r_sem, w1s_sem, w1r_sem, w1gs_sem, w1gr_sem):
     rows = x_ref.shape[0]
@@ -200,7 +200,7 @@
             for t in range(3):
                 self.third_copy(t).wait_send()
 
-    def phase(g, add, zero, finish, hook, first):
+    def phase(g, add, zero, finish, hook, first, whole=False):
         def a_wait(lo, hi):
             if first:
                 for i in range(lo, hi):
@@ -280,6 +280,10 @@
         add([(anti, 3)], 0, 9)
         g.sib_wait_last(3)
 
+        if whole:
+            finish(None, [(anti_sib, 3)])
+            return
+
         def last(m):
             @pl.when(m == UNITS - 1)
             def _():
@@ -310,17 +314,35 @@
     w2acc[:classes, :] = w2_ref[...]
     w2b[...] = w2acc[:cpad, :].astype(BF16)
 
-    def cnt_copy(i):
-        return remote(cnt_own, cnt_rcv.at[i], cs_sem.at[i], cr_sem.at[i], (me + i) % DEVICES)
+    partners = [sib] + nbr
+
+    def cnt_copy(k):
+        return remote(cnt_src.at[k], cnt_rcv.at[k], cs_sem.at[k], cr_sem.at[k], partners[k])
+
+    def cnt_next(k):
+        cnt_copy(k).wait_recv()
+        cnt_src[k + 1] = cnt_src[k] + cnt_rcv[k]
+        if k < 3:
+            cnt_copy(k + 1).start()
 
     local = jnp.sum(msk_ref[...].astype(F32), axis=1, keepdims=True)
     local = jnp.sum(local, axis=0, keepdims=True)
-    cnt_own[...] = jnp.broadcast_to(local, (8, LANES))
+    cnt_src[0] = jnp.broadcast_to(local, (8, LANES))
 
     def hook1(pre, i):
         if i is None:
             for j in range(8, DEVICES):
                 a_copy(j).start()
+            cnt_copy(0).start()
+            return
+
+        @pl.when(i == 1)
+        def _():
+            cnt_next(0)
+
+        @pl.when(i == 9)
+        def _():
+            cnt_next(1)
 
     def zero1():
         acc1[...] = jnp.zeros_like(acc1)
@@ -401,20 +423,17 @@
 
     def hook2(pre, i):
         if i is None:
-            for j in range(1, DEVICES):
-                cnt_copy(j).start()
             return
 
+        @pl.when(i == 0)
+        def _():
+            cnt_next(2)
+
         @pl.when(i == 9)
         def _():
-            for j in range(1, DEVICES):
-                cnt_copy(j).wait_recv()
-            total = cnt_own[...]
-            for j in range(1, DEVICES):
-                total = total + cnt_rcv[j]
-            cnt[...] = total
-            for j in range(1, DEVICES):
-                cnt_copy(j).wait_send()
+            cnt_next(3)
+            for k in range(4):
+                cnt_copy(k).wait_send()
 
     def finish2(m, pairs):
         s = mrows(m)
@@ -439,11 +458,15 @@
             mask = msk_ref[pl.ds(which, 1), :].astype(F32)
             picked = jnp.sum(jnp.where(hot, zc, 0.0), axis=0, keepdims=True)
             loss_acc[...] = loss_acc[...] + mask * (log_norm - picked)
-            gr = (jnp.exp(zm - log_norm) - jnp.where(hot, 1.0, 0.0)) * (mask / cnt[0:1, :])
+            gr = (jnp.exp(zm - log_norm) - jnp.where(hot, 1.0, 0.0)) * (mask / cnt_src[4][0:1, :])
             gb[uid(me, m), :, h * LANES:(h + 1) * LANES] = gr.astype(BF16)
         gg.start_own(m)
 
     phase(gh, add2, zero2, finish2, hook2, False)
+
+    def hook3(pre, i):
+        if i is None:
+            xt[...] = x_ref[...].T
 
     def finish3(m, pairs):
         s = mrows(m)
@@ -457,7 +480,7 @@
         gh.start_own(m)
 
     phase(gg, lambda pairs, t, k: add_cols(acc2, pairs, lambda j: gb[uid(*pairs[j])]), zero2, finish3,
-          lambda pre, i: None, False)
+          hook3, False)
 
     total_rows = w2acc.shape[0]
     half_rows = total_rows // 2
@@ -511,15 +534,12 @@
                 w2_scatter(j).start()
 
     def finish4(m, pairs):
-        s = mrows(m)
-        z = acc1[s, :]
+        z = acc1[...]
         for dev, q in pairs:
-            z = z + dot(a_v[s, rows_of(dev, q)], hb[rows_of(dev, q), :])
-        part = dot_tn(x_ref[s, :], z.astype(BF16))
-        w1p[...] = w1p[...] + part
-
-    w1p[...] = jnp.zeros_like(w1p)
-    phase(gh, lambda pairs, t, k: add_rows(acc1, pairs, lambda j: hb[rows_of(*pairs[j]), :]), zero1, finish4, hook4, False)
+            z = z + dot(a_v[:, rows_of(dev, q)], hb[rows_of(dev, q), :])
+        w1p[...] = dot(xt[...], z.astype(BF16))
+
+    phase(gh, lambda pairs, t, k: add_rows(acc1, pairs, lambda j: hb[rows_of(*pairs[j]), :]), zero1, finish4, hook4, False, True)
 
     sl = fin // DEVICES
 
@@ -540,6 +560,7 @@
 
     for i in range(1, DEVICES):
         w1_scatter(i).start()
+    gh.wait_sends()
     own = w2rows(core * half_rows + chip * piece, piece)
     total2 = w2acc[own, :]
     for j in range(1, chips):
@@ -568,7 +589,7 @@
         w2_gather(j, chip).wait_send()
     w2_sib_gather(1 - core).wait_recv()
     g2_out[...] = w2f[:classes, :]
-    loss_out[0, 0] = jnp.sum(w2f[total_rows - 1:, :LANES] / cnt[0:1, :])
+    loss_out[0, 0] = jnp.sum(w2f[total_rows - 1:, :LANES] / cnt_src[4][0:1, :])
     for i in range(1, DEVICES):
         w1_gather_in(i).wait_recv()
     g1_out[...] = w1f[...]
@@ -621,10 +642,10 @@
                 pltpu.VMEM((fin, hid), F32),
                 pltpu.VMEM((DEVICES, fin // DEVICES, hid), F32),
                 pltpu.VMEM((fin, hid), F32),
-                pltpu.VMEM((8, LANES), F32),
-                pltpu.VMEM((DEVICES, 8, LANES), F32),
-                pltpu.VMEM((8, LANES), F32),
+                pltpu.VMEM((5, 8, LANES), F32),
+                pltpu.VMEM((4, 8, LANES), F32),
                 pltpu.VMEM((1, LANES), F32),
+                pltpu.VMEM((fin, rows), BF16),
                 dma((DEVICES,)),
                 dma((2, 30)), dma((2, 30)), dma((2, 32)), dma((2, 32)),
                 dma((DEVICES,)), dma((DEVICES,)), dma((DEVICES,)), dma((DEVICES,)),

time: 149 us -> 148 us (level)
    pallas_call x1, Pallas kernels: 143 us -> 142 us  [local_step(): pl.pallas_call(functools.partial(step_kernel, classes), out_shape=(jax.Sh...]
where the time goes in v6:
time: 148 us; the launch traced here: 147 us
  Pallas kernels  142 us (96%)
  local copies, waits for them, and re-layouts  3.31 us (2%)
  between operations  2.38 us (2%)
    pallas_call x1, Pallas kernels, local_step(): pl.pallas_call(functools.partial(step_kernel, classes), out_shape=(jax.Sh...  142 us
    unnamed x2, local copies, waits for them, and re-layouts  3.31 us

profile of v6, /device:TPU:0, one launch (start us, length us, event | category | flops | bytes accessed | tf_op | source)
XLA Modules:
  0.0 147.4 jit_solution(17605563645757132792)
XLA Ops:
  0.6 141.7 %gcn_step.1 = (f32[1,1]{1,0:T(1,128)}, f32[128,256]{1,0:T(8,128)}, f32[349,256]{1,0:T(8,128)}) custom-call(bf16[1024,16384]{1,0:T(8,128)(2,1)} %adj.1, bf16[1024,128]{1,0:T(8,128)(2,1)} %x_hbm.1, f32[128,256]{1,0:T(8,128)} %w1_hbm.1, f32[349,256]{1,0:T(8,128)} %bitcast.6, s32[8,128]{1,0:T(8,128)} %bitcast.7, s32[8,128]{1,0:T(8,128)} %bitcast.8), custom_call_target="tpu_custom_call" | custom-call | tf_op jit(solution)/shard_map/gcn_step/pallas_call | solution.py:613
  143.0 1.6 %copy.13 = f32[128,256]{1,0:T(8,128)} copy(f32[128,256]{1,0:T(8,128)} %get-tuple-element.13) | data formatting | bytes 262144
  144.5 1.7 %copy.14 = f32[256,349]{0,1:T(8,128)} copy(f32[256,349]{0,1:T(8,128)} %bitcast.5) | data formatting | bytes 714752

commit v7 on v6

--- a/solution.py
+++ b/solution.py
@@ -34,13 +34,13 @@
 
 def step_kernel(classes, adj, x_hbm, w1_hbm, w2_hbm, lab_hbm, msk_hbm,
                 loss_out, g1_out, g2_out,
-                x_ref, w1_ref, w2_ref, lab_ref, msk_ref, in_sem,
-                a_v, gb, hb, acc1, acc2, ys1, ys2, hown, e2own, w1b, w2b,
+                w1_ref, w2_ref, lab_ref, msk_ref, in_sem,
+                a_v, gb, hb, acc1, acc2, ys, hown, w1b, w2b,
                 w2acc, w2rcv, w2part, w2f, w1p, w1r, w1f, cnt_src, cnt_rcv, loss_acc, xt,
                 a_sem, rsem, ssem, sib_rsem, sib_ssem, cs_sem, cr_sem,
                 w2s_sem, w2r_sem, w1s_sem, w1r_sem, w1gs_sem, w1gr_sem):
-    rows = x_ref.shape[0]
-    fin = x_ref.shape[1]
+    rows = x_hbm.shape[0]
+    fin = x_hbm.shape[1]
     unit = rows // UNITS
     hid = w1_ref.shape[1]
     cpad = w2b.shape[0]
@@ -86,7 +86,7 @@
     x_units = [pltpu.make_async_copy(x_hbm.at[pl.ds(q * unit, unit)], gb.at[uid(me, q), pl.ds(0, unit), pl.ds(0, fin)],
                                      in_sem.at[q]) for q in range(UNITS)]
     inputs = [pltpu.make_async_copy(src, dst, in_sem.at[UNITS + i]) for i, (src, dst) in enumerate(
-        [(w1_hbm, w1_ref), (w2_hbm, w2_ref), (msk_hbm, msk_ref), (lab_hbm, lab_ref), (x_hbm, x_ref)])]
+        [(w1_hbm, w1_ref), (w2_hbm, w2_ref), (msk_hbm, msk_ref), (lab_hbm, lab_ref)])]
     for c in x_units + inputs:
         c.start()
     for i in range(2):
@@ -242,14 +242,21 @@
                 for j in range(3):
                     g.arrive_last(j)
 
-            @pl.when(i == 9)
-            def _():
-                g.arrive_last(3)
+            if g.shared:
+                @pl.when(i == 9)
+                def _():
+                    g.arrive_last(3)
             hook(None, i)
 
             def half(t):
-                k = i - t
+                k = i - t if g.shared else i
                 hop, q, far = (k // 4) % 2, k % 4, k // 8
+
+                if not g.shared:
+                    @pl.when((t == 1) & (i == 8))
+                    def _():
+                        g.arrive_last(3)
+                        add([(anti, 3)], 0, 9)
 
                 @pl.when((k >= 0) & (k <= 8))
                 def _():
@@ -276,8 +283,12 @@
                         pairs.append((near_dev + far * (far_dev - near_dev), q + far * (r - q)))
                     add(pairs, t, k)
             halves(half)
-        loop(10, group)
-        add([(anti, 3)], 0, 9)
+        if g.shared:
+            loop(10, group)
+            add([(anti, 3)], 0, 9)
+        else:
+            loop(9, group)
+            hook(None, 9)
         g.sib_wait_last(3)
 
         if whole:
@@ -375,14 +386,14 @@
                 for r in range(3):
                     gx.sib_copy(me, 0, (back // 4) * 12 + r * 4 + back % 4).wait_send()
         for j, (dev, q) in enumerate(pairs):
-            ys1[at + j] = dot(gb[uid(dev, q), :unit, :fin], w1b[...]).astype(BF16)
+            ys[at + j, :unit, :hid] = dot(gb[uid(dev, q), :unit, :fin], w1b[...]).astype(BF16)
 
         def send():
             for j, (dev, q) in enumerate(pairs):
-                gx.sib_copy(dev, q, slots[j], ys1.at[at + j]).start()
+                gx.sib_copy(dev, q, slots[j], ys.at[at + j, pl.ds(0, unit), pl.ds(0, hid)]).start()
         if isinstance(k, int):
             send()
-        add_rows(acc1, pairs, lambda j: ys1[at + j])
+        add_rows(acc1, pairs, lambda j: ys[at + j, :unit, :hid])
         if not isinstance(k, int):
             send()
 
@@ -416,13 +427,15 @@
 
     def add2(pairs, t, k):
         for j, (dev, q) in enumerate(pairs):
-            ys2[j] = y2(dev, q)
-        add_cols(acc2, pairs, lambda j: ys2[j])
+            ys[j] = y2(dev, q)
+        add_cols(acc2, pairs, lambda j: ys[j])
 
     loss_acc[...] = jnp.zeros_like(loss_acc)
 
     def hook2(pre, i):
         if i is None:
+            for q in range(UNITS):
+                xt[:, q * unit:(q + 1) * unit] = gb[uid(me, q), :unit, :fin].T
             return
 
         @pl.when(i == 0)
@@ -441,10 +454,10 @@
         @pl.when(m == 0)
         def _():
             for j, (dev, q) in enumerate(pairs):
-                ys2[j] = y2(dev, q)
+                ys[j] = y2(dev, q)
         z = acc2[:, s]
         for j, (dev, q) in enumerate(pairs):
-            z = z + dot_nt(ys2[j], a_v[s, rows_of(dev, q)])
+            z = z + dot_nt(ys[j], a_v[s, rows_of(dev, q)])
         acc2[:, s] = z
         for h in range(unit // LANES):
             at = pl.ds(pl.multiple_of(m * unit + h * LANES, LANES), LANES)
@@ -464,23 +477,19 @@
 
     phase(gh, add2, zero2, finish2, hook2, False)
 
-    def hook3(pre, i):
-        if i is None:
-            xt[...] = x_ref[...].T
-
     def finish3(m, pairs):
         s = mrows(m)
         z = acc2[:, s]
         for dev, q in pairs:
             z = z + dot_nt(gb[uid(dev, q)], a_v[s, rows_of(dev, q)])
         e = z.astype(BF16)
-        e2own[:, s] = e
+        ys[m] = e
         gz = dot_tn(e, w2b[...])
         hb[rows_of(me, m), :] = jnp.where(acc1[s, :] > 0.0, gz, 0.0).astype(BF16)
         gh.start_own(m)
 
     phase(gg, lambda pairs, t, k: add_cols(acc2, pairs, lambda j: gb[uid(*pairs[j])]), zero2, finish3,
-          hook3, False)
+          lambda pre, i: None, False)
 
     total_rows = w2acc.shape[0]
     half_rows = total_rows // 2
@@ -514,7 +523,7 @@
     def hook4(pre, i):
         if i is None:
             w2acc[...] = jnp.zeros_like(w2acc)
-            w2acc[:cpad, :] = dot(e2own[...], hown[...])
+            w2acc[:cpad, :] = sum(dot(ys[q], hown[q * unit:(q + 1) * unit, :]) for q in range(UNITS))
             w2acc[total_rows - 1:, :LANES] = loss_acc[...]
             return
 
@@ -618,21 +627,18 @@
             in_specs=[pl.BlockSpec(memory_space=pl.ANY)] * 6,
             out_specs=(pl.BlockSpec(memory_space=pltpu.SMEM), vm, vm),
             scratch_shapes=[
-                pltpu.VMEM((rows, fin), BF16),
                 pltpu.VMEM((fin, hid), F32),
                 pltpu.VMEM((classes, hid), F32),
                 pltpu.VMEM((rows // LANES, LANES), jnp.int32),
                 pltpu.VMEM((rows // LANES, LANES), jnp.int32),
-                dma((UNITS + 5,)),
+                dma((UNITS + 4,)),
                 pltpu.VMEM((rows, nodes), BF16),
                 pltpu.VMEM((nodes // unit, cpad, unit), BF16),
                 pltpu.VMEM((nodes, hid), BF16),
                 pltpu.VMEM((rows, hid), F32),
                 pltpu.VMEM((cpad, rows), F32),
-                pltpu.VMEM((UNITS + 7, unit, hid), BF16),
-                pltpu.VMEM((UNITS, cpad, unit), BF16),
+                pltpu.VMEM((UNITS + 7, cpad, unit), BF16),
                 pltpu.VMEM((rows, hid), BF16),
-                pltpu.VMEM((cpad, rows), BF16),
                 pltpu.VMEM((fin, hid), BF16),
                 pltpu.VMEM((cpad, hid), BF16),
                 pltpu.VMEM((total_rows, hid), F32),

time: 148 us -> 148 us (level)
  no operation moved by 1% of the time
where the time goes in v7:
time: 148 us
  Pallas kernels  142 us (96%)
  local copies, waits for them, and re-layouts  3.31 us (2%)
  between operations  2.38 us (2%)
    pallas_call x1, Pallas kernels, local_step(): pl.pallas_call(functools.partial(step_kernel, classes), out_shape=(jax.Sh...  142 us
    unnamed x2, local copies, waits for them, and re-layouts  3.31 us

profile of v7, /device:TPU:0, one launch (start us, length us, event | category | flops | bytes accessed | tf_op | source)
XLA Modules:
  0.0 147.6 jit_solution(15958329866902909877)
XLA Ops:
  0.6 141.9 %gcn_step.1 = (f32[1,1]{1,0:T(1,128)}, f32[128,256]{1,0:T(8,128)}, f32[349,256]{1,0:T(8,128)}) custom-call(bf16[1024,16384]{1,0:T(8,128)(2,1)} %adj.1, bf16[1024,128]{1,0:T(8,128)(2,1)} %x_hbm.1, f32[128,256]{1,0:T(8,128)} %w1_hbm.1, f32[349,256]{1,0:T(8,128)} %bitcast.6, s32[8,128]{1,0:T(8,128)} %bitcast.7, s32[8,128]{1,0:T(8,128)} %bitcast.8), custom_call_target="tpu_custom_call" | custom-call | tf_op jit(solution)/shard_map/gcn_step/pallas_call | solution.py:622
  143.1 1.6 %copy.13 = f32[128,256]{1,0:T(8,128)} copy(f32[128,256]{1,0:T(8,128)} %get-tuple-element.13) | data formatting | bytes 262144
  144.7 1.7 %copy.14 = f32[256,349]{0,1:T(8,128)} copy(f32[256,349]{0,1:T(8,128)} %bitcast.5) | data formatting | bytes 714752

commit v8 on v7

--- a/solution.py
+++ b/solution.py
@@ -208,12 +208,12 @@
 
         zero()
 
-        def halves(fn):
+        def halves(fn, n=2):
             if g.shared:
                 fn(0)
                 fn(1)
             else:
-                loop(2, fn)
+                loop(n, fn)
 
         def near(t):
             if first and t == 0:
@@ -249,20 +249,24 @@
             hook(None, i)
 
             def half(t):
-                k = i - t if g.shared else i
+                if g.shared:
+                    k, sb, live = i - t, t, (i - t >= 0) & (i - t <= 8)
+                else:
+                    k, sb = i - t * (2 - t), (t + 1) // 2
+                    live = (t == 0) | ((t == 1) & (i >= 1) & (i <= 7)) | ((t == 2) & (i >= 7))
                 hop, q, far = (k // 4) % 2, k % 4, k // 8
 
                 if not g.shared:
-                    @pl.when((t == 1) & (i == 8))
+                    @pl.when((t == 2) & (i == 8))
                     def _():
                         g.arrive_last(3)
                         add([(anti, 3)], 0, 9)
 
-                @pl.when((k >= 0) & (k <= 8))
+                @pl.when(live)
                 def _():
                     def on_sib(cond, fn):
                         if not g.shared:
-                            pl.when((t == 1) & cond)(fn)
+                            pl.when((t >= 1) & cond)(fn)
                         elif t == 1:
                             pl.when(cond)(fn)
 
@@ -278,11 +282,11 @@
                     pairs = []
                     for r in range(3):
                         o, s = src_dev(me, own_d, hop, r), src_dev(sib, sib_d, hop, r)
-                        near_dev = o + t * (s - o)
-                        far_dev = anti + t * (anti_sib - anti)
+                        near_dev = o + sb * (s - o)
+                        far_dev = anti + sb * (anti_sib - anti)
                         pairs.append((near_dev + far * (far_dev - near_dev), q + far * (r - q)))
                     add(pairs, t, k)
-            halves(half)
+            halves(half, 3)
         if g.shared:
             loop(10, group)
             add([(anti, 3)], 0, 9)
@@ -536,7 +540,7 @@
             w2_sib().wait_recv()
             w2acc[mine, :] = w2acc[mine, :] + w2rcv[...]
 
-        @pl.when(i == 9)
+        @pl.when(i == 7)
         def _():
             w2_sib().wait_send()
             for j in range(1, chips):

time: 148 us -> 146 us (0.986)
  Pallas kernels: 142 us -> 140 us
    pallas_call x1, Pallas kernels: 142 us -> 140 us  [local_step(): pl.pallas_call(functools.partial(step_kernel, classes), out_shape=(jax.Sh...]
where the time goes in v8:
time: 146 us
  Pallas kernels  140 us (96%)
  local copies, waits for them, and re-layouts  3.31 us (2%)
  between operations  2.38 us (2%)
    pallas_call x1, Pallas kernels, local_step(): pl.pallas_call(functools.partial(step_kernel, classes), out_shape=(jax.Sh...  140 us
    unnamed x2, local copies, waits for them, and re-layouts  3.31 us

profile of v8, /device:TPU:0, one launch (start us, length us, event | category | flops | bytes accessed | tf_op | source)
XLA Modules:
  0.0 145.7 jit_solution(7969521382125528539)
XLA Ops:
  0.6 140.0 %gcn_step.1 = (f32[1,1]{1,0:T(1,128)}, f32[128,256]{1,0:T(8,128)}, f32[349,256]{1,0:T(8,128)}) custom-call(bf16[1024,16384]{1,0:T(8,128)(2,1)} %adj.1, bf16[1024,128]{1,0:T(8,128)(2,1)} %x_hbm.1, f32[128,256]{1,0:T(8,128)} %w1_hbm.1, f32[349,256]{1,0:T(8,128)} %bitcast.6, s32[8,128]{1,0:T(8,128)} %bitcast.7, s32[8,128]{1,0:T(8,128)} %bitcast.8), custom_call_target="tpu_custom_call" | custom-call | tf_op jit(solution)/shard_map/gcn_step/pallas_call | solution.py:626
  141.3 1.6 %copy.13 = f32[128,256]{1,0:T(8,128)} copy(f32[128,256]{1,0:T(8,128)} %get-tuple-element.13) | data formatting | bytes 262144
  142.8 1.7 %copy.14 = f32[256,349]{0,1:T(8,128)} copy(f32[256,349]{0,1:T(8,128)} %bitcast.5) | data formatting | bytes 714752

commit v9 on v8

--- a/solution.py
+++ b/solution.py
@@ -242,10 +242,6 @@
                 for j in range(3):
                     g.arrive_last(j)
 
-            if g.shared:
-                @pl.when(i == 9)
-                def _():
-                    g.arrive_last(3)
             hook(None, i)
 
             def half(t):
@@ -256,11 +252,13 @@
                     live = (t == 0) | ((t == 1) & (i >= 1) & (i <= 7)) | ((t == 2) & (i >= 7))
                 hop, q, far = (k // 4) % 2, k % 4, k // 8
 
+                def last_own():
+                    g.arrive_last(3)
+                    add([(anti, 3)], 0, 9)
                 if not g.shared:
-                    @pl.when((t == 2) & (i == 8))
-                    def _():
-                        g.arrive_last(3)
-                        add([(anti, 3)], 0, 9)
+                    pl.when((t == 2) & (i == 8))(last_own)
+                elif t == 1:
+                    pl.when(i == 8)(last_own)
 
                 @pl.when(live)
                 def _():
@@ -289,7 +287,6 @@
             halves(half, 3)
         if g.shared:
             loop(10, group)
-            add([(anti, 3)], 0, 9)
         else:
             loop(9, group)
             hook(None, 9)

time: 146 us -> 146 us (level)
  no operation moved by 1% of the time
where the time goes in v9:
time: 146 us
  Pallas kernels  140 us (96%)
  local copies, waits for them, and re-layouts  3.31 us (2%)
  between operations  2.38 us (2%)
    pallas_call x1, Pallas kernels, local_step(): pl.pallas_call(functools.partial(step_kernel, classes), out_shape=(jax.Sh...  140 us
    unnamed x2, local copies, waits for them, and re-layouts  3.31 us

profile of v9, /device:TPU:0, one launch (start us, length us, event | category | flops | bytes accessed | tf_op | source)
XLA Modules:
  0.0 145.9 jit_solution(5285931148752002651)
XLA Ops:
  0.6 140.2 %gcn_step.1 = (f32[1,1]{1,0:T(1,128)}, f32[128,256]{1,0:T(8,128)}, f32[349,256]{1,0:T(8,128)}) custom-call(bf16[1024,16384]{1,0:T(8,128)(2,1)} %adj.1, bf16[1024,128]{1,0:T(8,128)(2,1)} %x_hbm.1, f32[128,256]{1,0:T(8,128)} %w1_hbm.1, f32[349,256]{1,0:T(8,128)} %bitcast.6, s32[8,128]{1,0:T(8,128)} %bitcast.7, s32[8,128]{1,0:T(8,128)} %bitcast.8), custom_call_target="tpu_custom_call" | custom-call | tf_op jit(solution)/shard_map/gcn_step/pallas_call | solution.py:623
  141.4 1.6 %copy.13 = f32[128,256]{1,0:T(8,128)} copy(f32[128,256]{1,0:T(8,128)} %get-tuple-element.13) | data formatting | bytes 262144
  143.0 1.7 %copy.14 = f32[256,349]{0,1:T(8,128)} copy(f32[256,349]{0,1:T(8,128)} %bitcast.5) | data formatting | bytes 714752

commit v10 on v8

--- a/solution.py
+++ b/solution.py
@@ -559,19 +559,24 @@
     def w1rows(dev):
         return pl.ds(pl.multiple_of(dev * sl, sl), sl)
 
+    def flip(i):
+        return me + (i & 1) * (1 - 2 * core) + sum(((i >> (j + 1)) & 1) * step[j] for j in range(3))
+
+    far_first = sorted(range(1, DEVICES), key=lambda i: -bin(i >> 1).count("1"))
+
     def w1_scatter(i):
-        dev = (me + i) % DEVICES
+        dev = flip(i)
         return remote(w1p.at[w1rows(dev)], w1r.at[i], w1s_sem.at[i], w1r_sem.at[i], dev)
 
     def w1_gather(i):
-        dev = (me + i) % DEVICES
+        dev = flip(i)
         return remote(w1f.at[w1rows(me)], w1f.at[w1rows(me)], w1gs_sem.at[i], w1gr_sem.at[i], dev)
 
     def w1_gather_in(i):
-        dev = (me + DEVICES - i) % DEVICES
+        dev = flip(i)
         return remote(w1f.at[w1rows(dev)], w1f.at[w1rows(dev)], w1gs_sem.at[i], w1gr_sem.at[i], dev)
 
-    for i in range(1, DEVICES):
+    for i in far_first:
         w1_scatter(i).start()
     gh.wait_sends()
     own = w2rows(core * half_rows + chip * piece, piece)
@@ -593,7 +598,7 @@
     w1f[w1rows(me), :] = total
     for i in range(1, DEVICES):
         w1_scatter(i).wait_send()
-    for i in range(1, DEVICES):
+    for i in far_first:
         w1_gather(i).start()
     for j in range(1, chips):
         w2_gather(j, (chip + chips - j) % chips).wait_recv()

time: 146 us -> 145 us (level)
  no operation moved by 1% of the time
where the time goes in v10:
time: 145 us
  Pallas kernels  139 us (96%)
  local copies, waits for them, and re-layouts  3.31 us (2%)
  between operations  2.38 us (2%)
    pallas_call x1, Pallas kernels, local_step(): pl.pallas_call(functools.partial(step_kernel, classes), out_shape=(jax.Sh...  139 us
    unnamed x2, local copies, waits for them, and re-layouts  3.31 us

profile of v10, /device:TPU:0, one launch (start us, length us, event | category | flops | bytes accessed | tf_op | source)
XLA Modules:
  0.0 145.1 jit_solution(10194991181367832340)
XLA Ops:
  0.6 139.4 %gcn_step.1 = (f32[1,1]{1,0:T(1,128)}, f32[128,256]{1,0:T(8,128)}, f32[349,256]{1,0:T(8,128)}) custom-call(bf16[1024,16384]{1,0:T(8,128)(2,1)} %adj.1, bf16[1024,128]{1,0:T(8,128)(2,1)} %x_hbm.1, f32[128,256]{1,0:T(8,128)} %w1_hbm.1, f32[349,256]{1,0:T(8,128)} %bitcast.6, s32[8,128]{1,0:T(8,128)} %bitcast.7, s32[8,128]{1,0:T(8,128)} %bitcast.8), custom_call_target="tpu_custom_call" | custom-call | tf_op jit(solution)/shard_map/gcn_step/pallas_call | solution.py:631
  140.7 1.6 %copy.13 = f32[128,256]{1,0:T(8,128)} copy(f32[128,256]{1,0:T(8,128)} %get-tuple-element.13) | data formatting | bytes 262144
  142.3 1.7 %copy.14 = f32[256,349]{0,1:T(8,128)} copy(f32[256,349]{0,1:T(8,128)} %bitcast.5) | data formatting | bytes 714752
